TPU v7x, 256 devices: a whole 4x4x8 slice. The times are simulated.
256 devices in a mesh: band: 4 (over x), blk: 64 (over z, y, core).
Axes of the slice: x: 4, y: 4, z: 8, core: 2. Of those that a mesh axis runs over, the one named last changes fastest.
Arguments:
- solution: float32 [9, 2, 2048, 2048], P(None, None, 'blk', 'band'), may hold values from -6 to 6
- residual: float32 [9, 2, 2048, 2048], P(None, None, 'blk', 'band'), may hold values from -20 to 20
- direction: float32 [9, 2, 2048, 2048], P(None, None, 'blk', 'band'), may hold values from -20 to 20
- precond: float32 [9, 2048], P(None, 'band'), may hold values from 0.2 to 2
- inv_spec: float32 [9, 2048], P(None, 'band'), may hold values from 0.05 to 2
- mixing: float32 [9, 3], replicated, may hold values from 0.1 to 2.5
- beams: float32 [9, 2048], replicated, may hold values from 0.2 to 1
- slot_band: int32 [12], replicated, may hold values from 0 to 11, each once
- m_order: int32 [2048], replicated, may hold values from 0 to 2047, each once
- cycle_order: int32 [1024], replicated, may hold values from 0 to 1023, each once
- inv_noise: float32 [12, 3, 1024, 4096], P('band', None, 'blk'), may hold values from 0.3 to 3
- pix_mask: int32 [1024, 4096], P('blk'), may hold values 0 or 1
Outputs:
- solution_next: float32 [9, 2, 2048, 2048], P(None, None, 'blk', 'band')
- residual_next: float32 [9, 2, 2048, 2048], P(None, None, 'blk', 'band')
- direction_next: float32 [9, 2, 2048, 2048], P(None, None, 'blk', 'band')
Inputs may be any that keep to these rules, and one draw needn't show every extreme that they name: `slot_band`: slots holding a value of 9 or more are empty; each band lies in exactly one slot. `m_order`: each order 0 to 2047 appears once. `cycle_order`: each cycle 0 to 1023 appears once.
All inputs are finite; a program needn't handle non-finite values. No bound on the sum of `pix_mask` on one device may be relied on, other than what follows from the above.
Results may differ from a plain program's by a relative error of at most 0.0075.
Values may be sent and summed in bfloat16 or wider, within the bound.
A program may use at most 128 MiB of HBM per device.

v0:
```python
import functools
import math

import jax
import jax.numpy as jnp
from jax import lax
from jax.sharding import Mesh
from jax.sharding import PartitionSpec as P

COMP = 3
STOKES = 3
FIELDS = 9
BANDS = 9
SLOTS = 3
BLK = ("blk_0", "blk_1", "blk_2")
BAND_BLK = ("band", "blk_0", "blk_1", "blk_2")


def in_order(pieces, dim):
    pieces = jnp.moveaxis(pieces, 0, dim)
    shape = pieces.shape
    return pieces.reshape(*shape[:dim], shape[dim] * shape[dim + 1], *shape[dim + 2 :])


def copy_for_each(array, axis):
    devices = lax.axis_size(axis)
    return lax.all_to_all(
        jnp.broadcast_to(array[None], (devices, *array.shape)), axis, 0, 0, tiled=True
    )


def gathered_copies(array, axis, dim):
    return in_order(copy_for_each(array, axis), dim)


def cut_along(array, dim, devices):
    shape = array.shape
    pieces = array.reshape(*shape[:dim], devices, shape[dim] // devices, *shape[dim + 1 :])
    return jnp.moveaxis(pieces, dim, 0)


def sum_at_owner(array, axis, dim):
    devices = lax.axis_size(axis)
    pieces = lax.all_to_all(cut_along(array, dim, devices), axis, 0, 0, tiled=True)
    return jnp.sum(pieces.astype(jnp.float32), axis=0)


def by_axis(array, axes):
    return functools.reduce(lax.psum, axes, array)


def legendre_table(cycle_order, l_total, cycle_total):
    l_values = jnp.arange(l_total, dtype=jnp.int32)
    phase_int = l_values[None, :] * (2 * cycle_order[:, None] + 1) % (4 * cycle_total)
    angles = phase_int.astype(jnp.float32) * (math.pi / (2 * cycle_total))
    return (jnp.cos(angles) / math.sqrt(l_total)).astype(jnp.bfloat16)


def fourier_block(m_order, block_width, phi_total):
    phi_cells = jnp.arange(block_width, dtype=jnp.int32)
    phase_int = m_order[:, None] * phi_cells[None, :] % phi_total
    angles = phase_int.astype(jnp.float32) * (2.0 * math.pi / phi_total)
    scaling = 1.0 / math.sqrt(m_order.shape[0])
    return jnp.stack([jnp.cos(angles) * scaling, -jnp.sin(angles) * scaling]).astype(jnp.bfloat16)


def slot_tables(my_slots, mixing, beams):
    select = (my_slots[:, None] == jnp.arange(BANDS, dtype=jnp.int32)[None, :]).astype(jnp.float32)
    highest = lax.Precision.HIGHEST
    return (jnp.dot(select, mixing, precision=highest), jnp.dot(select, beams, precision=highest))


def band_amplitudes(rows_piece, slot_mix, slot_beam, orders):
    count = rows_piece.shape[3]
    l_values = jnp.arange(count, dtype=jnp.int32)
    triangle = (l_values[None, :] >= orders[:, None]).astype(jnp.float32)
    comp_data = rows_piece.astype(jnp.float32).reshape(COMP, STOKES, 2, orders.shape[0], count)
    mixed_sum = slot_mix[:, 0][:, None, None, None, None] * comp_data[0][None]
    for comp_index in range(1, COMP):
        mixed_sum = (
            mixed_sum
            + slot_mix[:, comp_index][:, None, None, None, None] * comp_data[comp_index][None]
        )
    return (mixed_sum * slot_beam[:, None, None, None, :] * triangle[None, None, None]).astype(
        jnp.bfloat16
    )


def sky_weights(cycle_side, m_order, weight):
    phi_total = weight.shape[3]
    block_width = phi_total // 4
    base = fourier_block(m_order, block_width, phi_total)
    turn_base = m_order % 4

    def fourier_turn(block_step, running):
        quarter = turn_base * block_step % 4
        cos_turn = jnp.where(quarter == 0, 1.0, jnp.where(quarter == 2, -1.0, 0.0)).astype(
            jnp.bfloat16
        )
        sin_turn = jnp.where(quarter == 1, 1.0, jnp.where(quarter == 3, -1.0, 0.0)).astype(
            jnp.bfloat16
        )
        real_row = base[0] * cos_turn[:, None] + base[1] * sin_turn[:, None]
        imag_row = base[1] * cos_turn[:, None] - base[0] * sin_turn[:, None]
        azim = jnp.stack([real_row, imag_row])
        sky_part = jnp.einsum(
            "sxrkm,kmp->sxrp", cycle_side, azim, preferred_element_type=jnp.float32
        )
        noise_part = lax.dynamic_slice_in_dim(weight, block_step * block_width, block_width, 3)
        weighted = (noise_part * sky_part).astype(jnp.bfloat16)
        return running + jnp.einsum(
            "sxrp,kmp->sxrkm", weighted, azim, preferred_element_type=jnp.float32
        )

    running = lax.fori_loop(0, 4, fourier_turn, jnp.zeros(cycle_side.shape, jnp.float32))
    return running.astype(jnp.bfloat16)


def combine_bands(returned, colat, slot_mix, slot_beam, orders):
    back_harm = jnp.einsum("sxrkm,rl->sxkml", returned, colat, preferred_element_type=jnp.float32)
    l_total = colat.shape[1]
    triangle = (jnp.arange(l_total, dtype=jnp.int32)[None, :] >= orders[:, None]).astype(
        jnp.float32
    )
    back_harm = back_harm * slot_beam[:, None, None, None, :] * triangle[None, None, None]
    pieces = [
        jnp.sum(slot_mix[:, comp_index][:, None, None, None, None] * back_harm, axis=0)
        for comp_index in range(COMP)
    ]
    return jnp.stack(pieces).reshape(FIELDS, 2, orders.shape[0], l_total)


def on_device(
    solution,
    residual,
    direction,
    precond,
    inv_spec,
    mixing,
    beams,
    slot_band,
    m_order,
    cycle_order,
    inv_noise,
    pix_mask,
):
    band_index = lax.axis_index("band")
    block_index = lax.axis_index(BLK)
    band_count = lax.axis_size("band")
    m_local = direction.shape[2]
    l_local = direction.shape[3]
    colat = legendre_table(cycle_order, l_local * band_count, cycle_order.shape[0])
    my_orders = lax.dynamic_slice_in_dim(m_order, block_index * m_local, m_local)
    halved = direction.astype(jnp.bfloat16)
    weight = inv_noise * pix_mask.astype(jnp.float32)[None, None]
    my_slots = lax.dynamic_slice_in_dim(slot_band, band_index * SLOTS, SLOTS)
    slot_mix, slot_beam = slot_tables(my_slots, mixing, beams)
    amplitudes = band_amplitudes(gathered_copies(halved, "band", 3), slot_mix, slot_beam, my_orders)
    colat_side = jnp.einsum(
        "sxkml,rl->sxrkm", amplitudes, colat, preferred_element_type=jnp.float32
    ).astype(jnp.bfloat16)
    cycle_side = lax.all_to_all(colat_side, BLK, split_axis=2, concat_axis=4, tiled=True)
    weighted_back = sky_weights(cycle_side, m_order, weight)
    returned = lax.all_to_all(weighted_back, BLK, split_axis=4, concat_axis=2, tiled=True)
    combined = combine_bands(returned, colat, slot_mix, slot_beam, my_orders)
    data_term = sum_at_owner(combined.astype(jnp.bfloat16), "band", 3)
    prior_diag = inv_spec[:, None, None, :]
    precond_full = precond[:, None, None, :]
    applied = prior_diag * direction + data_term
    scaled_res = precond_full * residual
    norm_old, curvature, crossed, squared = (
        by_axis(jnp.sum(residual * scaled_res), BAND_BLK),
        by_axis(jnp.sum(direction * applied), BAND_BLK),
        by_axis(jnp.sum(applied * scaled_res), BAND_BLK),
        by_axis(jnp.sum(applied * precond_full * applied), BAND_BLK),
    )
    step_size = norm_old / curvature
    solution_next = solution + step_size * direction
    residual_next = residual - step_size * applied
    scaled_next = precond_full * residual_next
    norm_new = norm_old - 2.0 * step_size * crossed + step_size * step_size * squared
    direction_next = scaled_next + norm_new / norm_old * direction
    return (solution_next, residual_next, direction_next)


def solution(mesh):
    finer = Mesh(
        mesh.devices.reshape(mesh.shape["band"], 8, 4, 2), ("band", "blk_0", "blk_1", "blk_2")
    )
    in_specs = (
        P(None, None, BLK, "band"),
        P(None, None, BLK, "band"),
        P(None, None, BLK, "band"),
        P(None, "band"),
        P(None, "band"),
        P(),
        P(),
        P(),
        P(),
        P(),
        P("band", None, BLK, None),
        P(BLK, None),
    )
    out_specs = (P(None, None, BLK, "band"), P(None, None, BLK, "band"), P(None, None, BLK, "band"))
    return jax.shard_map(
        on_device, mesh=finer, in_specs=in_specs, out_specs=out_specs, check_vma=False
    )
```

profile of v0, /device:TPU:1, one launch (start us, length us, event | category | flops | bytes accessed | tf_op | source)
XLA Modules:
  0.0 463.7 jit_solution(5696534345830103416)
XLA Ops:
  3.8 4.8 %all-to-all-start = ((bf16[4,9,2,32,512]{4,3,2,1,0:T(8,128)(2,1)}), bf16[4,9,2,32,512]{4,3,2,1,0:T(8,128)(2,1)S(1)}, u32[]{:S(2)}, u32[]{:S(2)}) async-start(bf16[4,9,2,32,512]{4,3,2,1,0:T(8,128)(2,1)} %broadcast_in_dim.34), calls=%async_computation | async-start | bytes 4718592 | tf_op jit(solution)/shard_map/all_to_all | solution.py:27
  9.4 26.5 %all-to-all-done = bf16[4,9,2,32,512]{4,3,2,1,0:T(8,128)(2,1)S(1)} async-done(((bf16[4,9,2,32,512]{4,3,2,1,0:T(8,128)(2,1)}), bf16[4,9,2,32,512]{4,3,2,1,0:T(8,128)(2,1)S(1)}, u32[]{:S(2)}, u32[]{:S(2)}) %all-to-all-start) | async-done | bytes 2359328 | tf_op jit(solution)/shard_map/all_to_all | solution.py:27
  39.4 32.8 %fusion.47 = bf16[3,3,1024,2,32]{2,4,3,1,0:T(8,128)(2,1)S(1)} fusion(s32[1024]{0:T(1024)S(1)} %multiply_add_fusion.4, bf16[3,3,2,32,2048]{4,3,2,1,0:T(8,128)(2,1)S(1)} %multiply_convert_fusion.11), kind=kOutput, calls=%fused_computation.74 | convolution fusion | flops 2450063360 | bytes 3543040 | tf_op jit(solution)/shard_map/sxkml,rl->sxrkm/dot_general | solution.py:159
  72.1 8.5 %copy.32 = bf16[3,3,1024,2,32]{4,3,1,0,2:T(2,128)(2,1)} copy(bf16[3,3,1024,2,32]{2,4,3,1,0:T(8,128)(2,1)S(1)} %fusion.47) | data formatting | bytes 2359296 | tf_op jit(solution)/shard_map/convert_element_type | solution.py:161
  80.6 11.2 %reshape.226 = bf16[64,2,4608]{2,1,0:T(2,128)(2,1)} reshape(bf16[1024,3,3,2,32]{4,3,2,1,0:T(2,128)(2,1)} %bitcast.118) | data formatting | bytes 2359296
  91.8 14.5 %all-to-all-start.1 = ((bf16[64,2,4608]{2,1,0:T(2,128)(2,1)}), bf16[64,2,4608]{2,1,0:T(2,128)(2,1)S(1)}, u32[]{:S(2)}, u32[]{:S(2)}) async-start(bf16[64,2,4608]{2,1,0:T(2,128)(2,1)} %reshape.226), calls=%async_computation.1 | async-start | bytes 2359296 | tf_op jit(solution)/shard_map/all_to_all | solution.py:162
  106.3 36.1 %multiply_convert_fusion.1 = (bf16[1,2048,1024]{2,1,0:T(8,128)(2,1)S(1)}, bf16[1,2048,1024]{2,1,0:T(8,128)(2,1)}) fusion(s32[2048]{0:T(1024)S(1)} %copy-done.14), kind=kLoop, calls=%fused_computation.37 | loop fusion | flops 39845888 | bytes 8396800 | tf_op jit(solution)/shard_map/convert.7
  142.4 6.2 %pad_maximum_fusion = bf16[2,2048,1024]{2,1,0:T(8,128)(2,1)} fusion(bf16[1,2048,1024]{2,1,0:T(8,128)(2,1)} %get-tuple-element.233, bf16[1,2048,1024]{2,1,0:T(8,128)(2,1)S(1)} %get-tuple-element.232), kind=kLoop, calls=%fused_computation.33 | loop fusion | flops 4194304 | bytes 16777216 | tf_op jit(solution)/shard_map/stack | solution.py:64
  162.6 7.7 %all_to_all.36 = bf16[3,3,16,2,2048]{4,2,3,1,0:T(8,128)(2,1)} reshape(bf16[3,3,16,2,64,32]{5,4,2,3,1,0:T(8,128)(2,1)} %copy.34) | data formatting | bytes 2359296 | tf_op jit(solution)/shard_map/all_to_all | solution.py:162
  170.3 41.1 %while.16 = (s32[]{:T(128)}, f32[3,3,16,2,2048]{4,2,3,1,0:T(8,128)S(1)}, f32[3,3,16,4096]{3,2,1,0:T(8,128)}, bf16[2,2048,1024]{2,1,0:T(8,128)(2,1)}, s32[2048]{0...) while((s32[]{:T(128)}, ...), condition=%wide.region_6.7_spmd.clone, body=%wide.region_5.6_spmd.clone.sunk | while | flops 2463576064 | bytes 45375684 | solution.py:115
  170.3 4.1 multiply_add_fusion.7
  180.6 4.1 multiply_add_fusion.7
  201.2 4.1 multiply_add_fusion.7
  214.6 16.8 %copy.35 = bf16[3,3,16,2,2048]{2,3,1,0,4:T(2,128)(2,1)} copy(bf16[3,3,16,2,2048]{4,2,3,1,0:T(8,128)(2,1)S(1)} %convert_element_type.112) | data formatting | bytes 2359296 | tf_op jit(solution)/shard_map/convert_element_type | solution.py:116
  231.4 26.0 %reshape.228 = bf16[64,2,4608]{2,1,0:T(2,128)(2,1)S(1)} reshape(bf16[2048,3,3,2,16]{4,3,2,1,0:T(2,128)(2,1)} %bitcast.116) | data formatting | bytes 2359296
  257.4 40.7 %all_to_all.46 = bf16[64,2,4608]{2,1,0:T(2,128)(2,1)S(1)} all-to-all(bf16[64,2,4608]{2,1,0:T(2,128)(2,1)S(1)} %reshape.228), channel_id=1, replica_groups=mesh['band'=4,'blk_0'=8,'blk_1'=4,'blk_2'=2] {'blk_0','blk_1','blk_2'}, dimensions={0} | all-to-all | bytes 2359296 | tf_op jit(solution)/shard_map/all_to_all | solution.py:164
  298.1 8.1 %reshape.229 = bf16[2048,3,3,2,16]{4,3,2,1,0:T(2,128)(2,1)} reshape(bf16[64,2,4608]{2,1,0:T(2,128)(2,1)S(1)} %all_to_all.46) | data formatting | bytes 2359296
  306.3 20.3 %copy.46 = bf16[3,3,16,2,64,32]{5,2,4,3,1,0:T(8,128)(2,1)} copy(bf16[3,3,16,2,64,32]{2,3,1,0,5,4:T(2,128)(2,1)} %bitcast.117) | data formatting | bytes 2359296 | tf_op jit(solution)/shard_map/all_to_all | solution.py:164
  326.6 48.8 %multiply_reduce_fusion.2 = (bf16[3,2,32,2048]{3,2,1,0:T(8,128)(2,1)S(1)}, bf16[3,2,32,2048]{3,2,1,0:T(8,128)(2,1)S(1)}, bf16[3,2,32,2048]{3,2,1,0:T(8,128)(2,1)S(1)}) fusion(f32[32,2048]{1,0:T(8,128)S(1)} %copy-done.8, f32[3,2048]{1,0:T(4,128)S(1)} %copy-done.12, f32[3]{0:T(128)S(1)} %copy-done.17, f32[3]{0:T(128)S(1)} %copy-done.21, f32[3]{0:T(128)S(1)} %copy-done.19, ...), kind=kOutput, calls=%fused_computation.46 | convolution fusion | flops 2457731072 | bytes 3829796 | tf_op jit(solution)/shard_map/sxrkm,rl->sxkml/dot_general | solution.py:120
  381.0 30.1 %all_to_all.47 = bf16[4,9,2,32,512]{4,3,2,1,0:T(8,128)(2,1)S(1)} all-to-all(bf16[4,9,2,32,512]{4,3,2,1,0:T(8,128)(2,1)S(1)} %copy.39), channel_id=1, replica_groups=mesh['band'=4,'blk_0'=8,'blk_1'=4,'blk_2'=2] {'band'}, dimensions={0} | all-to-all | bytes 4718592 | tf_op jit(solution)/shard_map/all_to_all | solution.py:44
  413.7 7.6 %all-reduce.2 = (f32[]{:T(128)}, f32[]{:T(128)}, f32[]{:T(128)}, f32[]{:T(128)}) all-reduce(f32[]{:T(128)} %get-tuple-element.191, f32[]{:T(128)} %get-tuple-element.192, f32[]{:T(128)} %get-tuple-element.190, f32[]{:T(128)} %get-tuple-element.189), channel_id=1, replica_groups=mesh['band'=4,'blk_0'=8,'blk_1'=4,'blk_2'=2] {'band'}, use_global_device_ids=true, to_apply=%region_1.2 | all-reduce | flops 4 | bytes 32 | tf_op jit(solution)/shard_map/psum | solution.py:49
  421.3 14.9 %all-reduce = (f32[]{:T(128)}, f32[]{:T(128)}, f32[]{:T(128)}, f32[]{:T(128)}) all-reduce(f32[]{:T(128)} %get-tuple-element.213, f32[]{:T(128)} %get-tuple-element.214, f32[]{:T(128)} %get-tuple-element.215, f32[]{:T(128)} %get-tuple-element.216), channel_id=1, replica_groups=mesh['band'=4,'blk_0'=8,'blk_1'=4,'blk_2'=2] {'blk_0'}, use_global_device_ids=true, to_apply=%region_2.3 | all-reduce | flops 4 | bytes 32 | tf_op jit(solution)/shard_map/psum | solution.py:49
  436.2 7.3 %all-reduce.1 = (f32[]{:T(128)}, f32[]{:T(128)}, f32[]{:T(128)}, f32[]{:T(128)}) all-reduce(f32[]{:T(128)} %get-tuple-element.205, f32[]{:T(128)} %get-tuple-element.206, f32[]{:T(128)} %get-tuple-element.207, f32[]{:T(128)} %get-tuple-element.208), channel_id=1, replica_groups=mesh['band'=4,'blk_0'=8,'blk_1'=4,'blk_2'=2] {'blk_1'}, use_global_device_ids=true, to_apply=%region_3.4 | all-reduce | flops 4 | bytes 32 | tf_op jit(solution)/shard_map/psum | solution.py:49
  443.4 12.4 %all-reduce.3 = (f32[]{:T(128)}, f32[]{:T(128)}, f32[]{:T(128)}, f32[]{:T(128)}) all-reduce(f32[]{:T(128)} %get-tuple-element.209, f32[]{:T(128)} %get-tuple-element.210, f32[]{:T(128)} %get-tuple-element.211, f32[]{:T(128)} %get-tuple-element.212), channel_id=1, replica_groups=mesh['band'=4,'blk_0'=8,'blk_1'=4,'blk_2'=2] {'blk_2'}, use_global_device_ids=true, to_apply=%region_4.5 | all-reduce | flops 4 | bytes 32 | tf_op jit(solution)/shard_map/psum | solution.py:49
  (97 shorter events, 64.9 us)
Async XLA Ops:
  0.6 8.5 %copy-start = (f32[9,2048]{1,0:T(8,128)S(1)}, f32[9,2048]{1,0:T(8,128)}, u32[]{:S(2)}) copy-start(f32[9,2048]{1,0:T(8,128)} %param.20) | copy-start | bytes 221188
  2.0 6.6 %copy-start.9 = (s32[16,4096]{1,0:T(8,128)S(1)}, s32[16,4096]{1,0:T(8,128)}, u32[]{:S(2)}) copy-start(s32[16,4096]{1,0:T(8,128)} %param.25) | copy-start | bytes 786436
  2.1 6.6 %copy-start.14 = (s32[2048]{0:T(1024)S(1)}, s32[2048]{0:T(1024)}, u32[]{:S(2)}) copy-start(s32[2048]{0:T(1024)} %param.22) | copy-start | bytes 24580
  2.1 6.7 %copy-start.23 = (s32[12]{0:T(128)S(1)}, s32[12]{0:T(128)}, u32[]{:S(2)}) copy-start(s32[12]{0:T(128)} %param.21) | copy-start | bytes 148
  2.1 6.8 %copy-start.22 = (f32[9,3]{0,1:T(4,128)S(1)}, f32[9,3]{0,1:T(4,128)}, u32[]{:S(2)}) copy-start(f32[9,3]{0,1:T(4,128)} %param.19) | copy-start | bytes 328
  2.1 6.9 %copy-start.15 = (s32[1024]{0:T(1024)S(1)}, s32[1024]{0:T(1024)}, u32[]{:S(2)}) copy-start(s32[1024]{0:T(1024)} %param.23) | copy-start | bytes 12292
  3.8 32.1 %all-to-all-start = ((bf16[4,9,2,32,512]{4,3,2,1,0:T(8,128)(2,1)}), bf16[4,9,2,32,512]{4,3,2,1,0:T(8,128)(2,1)S(1)}, u32[]{:S(2)}, u32[]{:S(2)}) async-start(bf16[4,9,2,32,512]{4,3,2,1,0:T(8,128)(2,1)} %broadcast_in_dim.34), calls=%async_computation | async-start | bytes 4718592 | tf_op jit(solution)/shard_map/all_to_all | solution.py:27
  9.0 29.0 %copy-start.16 = (f32[3]{0:T(128)}, f32[3]{0:T(128)S(1)}, u32[]{:S(2)}) copy-start(f32[3]{0:T(128)S(1)} %get-tuple-element.234) | copy-start | bytes 40
  9.1 29.0 %copy-start.18 = (f32[3]{0:T(128)}, f32[3]{0:T(128)S(1)}, u32[]{:S(2)}) copy-start(f32[3]{0:T(128)S(1)} %get-tuple-element.235) | copy-start | bytes 40
  9.1 29.0 %copy-start.20 = (f32[3]{0:T(128)}, f32[3]{0:T(128)S(1)}, u32[]{:S(2)}) copy-start(f32[3]{0:T(128)S(1)} %get-tuple-element.236) | copy-start | bytes 40
  9.3 28.7 %copy-start.11 = (f32[3,2048]{1,0:T(4,128)}, f32[3,2048]{1,0:T(4,128)S(1)}, u32[]{:S(2)}) copy-start(f32[3,2048]{1,0:T(4,128)S(1)} %fusion.55) | copy-start | bytes 73732
  9.4 28.6 %copy-start.7 = (f32[32,2048]{1,0:T(8,128)}, f32[32,2048]{1,0:T(8,128)S(1)}, u32[]{:S(2)}) copy-start(f32[32,2048]{1,0:T(8,128)S(1)} %fusion.53) | copy-start | bytes 786436
  91.8 60.0 %all-to-all-start.1 = ((bf16[64,2,4608]{2,1,0:T(2,128)(2,1)}), bf16[64,2,4608]{2,1,0:T(2,128)(2,1)S(1)}, u32[]{:S(2)}, u32[]{:S(2)}) async-start(bf16[64,2,4608]{2,1,0:T(2,128)(2,1)} %reshape.226), calls=%async_computation.1 | async-start | bytes 2359296 | tf_op jit(solution)/shard_map/all_to_all | solution.py:162
  162.6 7.7 %copy-start.4 = (f32[3,3,16,2,2048]{4,2,3,1,0:T(8,128)S(1)}, f32[3,3,16,2,2048]{4,2,3,1,0:T(8,128)}, u32[]{:S(2)}) copy-start(f32[3,3,16,2,2048]{4,2,3,1,0:T(8,128)} %custom-call) | copy-start | bytes 7077892
  306.2 20.3 %copy-start.8 = (f32[32,2048]{1,0:T(8,128)S(1)}, f32[32,2048]{1,0:T(8,128)}, u32[]{:S(2)}) copy-start(f32[32,2048]{1,0:T(8,128)} %copy-done.7) | copy-start | bytes 786436
  306.2 20.3 %copy-start.12 = (f32[3,2048]{1,0:T(4,128)S(1)}, f32[3,2048]{1,0:T(4,128)}, u32[]{:S(2)}) copy-start(f32[3,2048]{1,0:T(4,128)} %copy-done.11) | copy-start | bytes 73732
  306.2 20.3 %copy-start.17 = (f32[3]{0:T(128)S(1)}, f32[3]{0:T(128)}, u32[]{:S(2)}) copy-start(f32[3]{0:T(128)} %copy-done.16) | copy-start | bytes 40
  306.2 20.3 %copy-start.19 = (f32[3]{0:T(128)S(1)}, f32[3]{0:T(128)}, u32[]{:S(2)}) copy-start(f32[3]{0:T(128)} %copy-done.18) | copy-start | bytes 40
  306.2 20.3 %copy-start.21 = (f32[3]{0:T(128)S(1)}, f32[3]{0:T(128)}, u32[]{:S(2)}) copy-start(f32[3]{0:T(128)} %copy-done.20) | copy-start | bytes 40
  380.9 30.6 %copy-start.2 = (f32[9,2,32,512]{3,2,1,0:T(8,128)S(1)}, f32[9,2,32,512]{3,2,1,0:T(8,128)}, u32[]{:S(2)}) copy-start(f32[9,2,32,512]{3,2,1,0:T(8,128)} %param.16) | copy-start | bytes 3538948
  380.9 30.6 %copy-start.3 = (f32[9,2,32,512]{3,2,1,0:T(8,128)S(1)}, f32[9,2,32,512]{3,2,1,0:T(8,128)}, u32[]{:S(2)}) copy-start(f32[9,2,32,512]{3,2,1,0:T(8,128)} %param.15) | copy-start | bytes 3538948
  380.9 30.6 %copy-start.10 = (f32[9,512]{1,0:T(8,128)S(1)}, f32[9,512]{1,0:T(8,128)}, u32[]{:S(2)}) copy-start(f32[9,512]{1,0:T(8,128)} %param.17) | copy-start | bytes 55300
  381.0 30.6 %copy-start.13 = (f32[9,512]{1,0:T(8,128)S(1)}, f32[9,512]{1,0:T(8,128)}, u32[]{:S(2)}) copy-start(f32[9,512]{1,0:T(8,128)} %param.18) | copy-start | bytes 55300
  411.5 52.0 %copy-start.1 = (f32[9,2048]{1,0:T(8,128)S(1)}, f32[9,2048]{1,0:T(8,128)}, u32[]{:S(2)}) copy-start(f32[9,2048]{1,0:T(8,128)} %param.20) | copy-start | bytes 221188
  (5 other events, 18.1 us)
where the time goes:
time: 468 us; the launch traced here: 464 us
  local copies, waits for them, and re-layouts  119 us (25%)
  blocking collectives  113 us (24%)
  matrix products  106 us (23%)
  other arithmetic  74.2 us (16%)
  waiting for transfers between devices  26.5 us (6%)
  starting transfers between devices  19.3 us (4%)
  between operations  5.03 us (1%)
    unnamed x51, local copies, waits for them, and re-layouts  51.8 us
    dot_general x1, matrix products, combine_bands(): jnp.einsum('sxrkm,rl->sxkml', returned, colat, preferred_element_type=jnp...  48.8 us
    psum x4, blocking collectives, by_axis(): return functools.reduce(lax.psum, axes, array)  42.2 us
    all_to_all x1, blocking collectives, on_device(): lax.all_to_all(weighted_back, BLK, split_axis=4, concat_axis=2, tiled=True)  40.7 us
    another operation x1, other arithmetic  36.1 us
    dot_general x1, matrix products, on_device(): jnp.einsum('sxkml,rl->sxrkm', amplitudes, colat, preferred_element_type=j...  32.8 us
    all_to_all x1, blocking collectives, sum_at_owner(): lax.all_to_all(cut_along(array, dim, devices), axis, 0, 0, tiled=True)  30.1 us
    all_to_all x1, waiting for transfers between devices, copy_for_each(): lax.all_to_all(jnp.broadcast_to(array[None], (devices, *array.shape)), ax...  26.5 us
  transfers between devices with their start and end apart: 2, of which 1 were waited for; matrix products, arithmetic and copies ran while one was open for 10% of the time, Pallas kernels for 0%

commit v1 on v0

v1 whole, which is shorter than its diff:
```python
import functools
import math

import jax
import jax.numpy as jnp
from jax import lax
from jax.experimental import pallas as pl
from jax.experimental.pallas import tpu as pltpu
from jax.sharding import Mesh
from jax.sharding import PartitionSpec as P

COMP = 3
STOKES = 3
FIELDS = 9
BANDS = 9
SLOTS = 3
PAIRS = SLOTS * STOKES
L = 2048
CYCLES = 1024
MODES = 2048
PHI = 4096
QUARTER = PHI // 4
M_DEV = 32
R_DEV = 16
BLOCKS = 64
L_DEV = 512
LANES = PAIRS * 2 * M_DEV
BLK = ("blk_0", "blk_1", "blk_2")
BAND_BLK = ("band", "blk_0", "blk_1", "blk_2")
SCALE = 1.0 / math.sqrt(2048)
VMEM = pltpu.VMEM
F32 = jnp.float32
BF16 = jnp.bfloat16
NT = (((1,), (1,)), ((), ()))
NN = (((1,), (0,)), ((), ()))


def in_vmem():
    return pl.BlockSpec(memory_space=VMEM)


def in_smem():
    return pl.BlockSpec(memory_space=pltpu.SMEM)


def unit_circle(turn):
    half = (((turn + 2048) & 4095) - 2048).astype(F32) * (math.pi / 4096)
    sq = half * half
    sine = half * (
        1
        + sq
        * (-1 / 6 + sq * (1 / 120 + sq * (-1 / 5040 + sq * (1 / 362880 + sq * (-1 / 39916800)))))
    )
    cosine = 1 + sq * (
        -1 / 2
        + sq
        * (
            1 / 24
            + sq * (-1 / 720 + sq * (1 / 40320 + sq * (-1 / 3628800 + sq * (1 / 479001600))))
        )
    )
    return cosine * cosine - sine * sine, 2 * sine * cosine


def first_turns(mult):
    lane = lax.broadcasted_iota(jnp.int32, mult.shape, 1)
    cosine, sine = unit_circle((mult * lane) & 4095)
    step_cos, step_sin = unit_circle((mult * 128) & 4095)
    return cosine * SCALE, sine * SCALE, step_cos, step_sin


def colat_rows(mult, store):
    cosine, sine, step_cos, step_sin = first_turns(mult)
    for tile in range(L // 128):
        store(tile, cosine.astype(BF16))
        cosine, sine = cosine * step_cos - sine * step_sin, sine * step_cos + cosine * step_sin


def azim_rows(mult, store):
    cosine, sine, step_cos, step_sin = first_turns(mult)
    for tile in range(QUARTER // 128):
        store(tile, cosine.astype(BF16), (-sine).astype(BF16))
        cosine, sine = cosine * step_cos - sine * step_sin, sine * step_cos + cosine * step_sin


def tables_kernel(cycle_mult, order_mult, colat, azim):
    @pl.loop(0, cycle_mult.shape[0] // 32)
    def _(block):
        rows = pl.ds(pl.multiple_of(block * 32, 32), 32)

        def put(tile, value):
            colat[rows, tile * 128 : (tile + 1) * 128] = value

        colat_rows(cycle_mult[rows, :], put)

    @pl.loop(0, order_mult.shape[0] // 32)
    def _(block):
        rows = pl.ds(pl.multiple_of(block * 32, 32), 32)
        real_rows = pl.ds(pl.multiple_of(block * 64, 32), 32)
        imag_rows = pl.ds(pl.multiple_of(block * 64 + 32, 32), 32)

        def put(tile, real, imag):
            azim[real_rows, tile * 128 : (tile + 1) * 128] = real
            azim[imag_rows, tile * 128 : (tile + 1) * 128] = imag

        azim_rows(order_mult[rows, :], put)


def make_tables(cycle_mult, order_mult):
    steps = 8
    return pl.pallas_call(
        tables_kernel,
        grid=(steps,),
        in_specs=[
            pl.BlockSpec((CYCLES // steps, 128), lambda g: (g, 0)),
            pl.BlockSpec((MODES // steps, 128), lambda g: (g, 0)),
        ],
        out_specs=[
            pl.BlockSpec((CYCLES // steps, L), lambda g: (g, 0)),
            pl.BlockSpec((2 * MODES // steps, QUARTER), lambda g: (g, 0)),
        ],
        out_shape=[
            jax.ShapeDtypeStruct((CYCLES, L), BF16),
            jax.ShapeDtypeStruct((2 * MODES, QUARTER), BF16),
        ],
        cost_estimate=pl.CostEstimate(
            flops=60_000_000, bytes_accessed=14_000_000, transcendentals=0
        ),
        name="tables",
    )(cycle_mult, order_mult)


def at_least(orders, first, width):
    l_values = first + lax.broadcasted_iota(jnp.int32, (M_DEV, width), 1)
    return (l_values >= orders).astype(F32)


def forward_kernel(pieces, colat, beam, orders, mix, out, amps):
    for piece in range(4):
        for half in range(2):
            first = piece * L_DEV + half * 256
            cols = slice(half * 256, half * 256 + 256)
            triangle = at_least(orders[:, 0:1], first, 256)
            for s in range(STOKES):
                for k in range(2):
                    comps = [
                        pieces[piece, c * 3 + s, k, :, cols].astype(F32) for c in range(COMP)
                    ]
                    for x in range(SLOTS):
                        mixed = mix[x, 0] * comps[0]
                        for c in range(1, COMP):
                            mixed = mixed + mix[x, c] * comps[c]
                        row = ((s * 3 + x) * 2 + k) * M_DEV
                        value = mixed * beam[x : x + 1, first : first + 256] * triangle
                        amps[row : row + M_DEV, first : first + 256] = value.astype(BF16)

    @pl.loop(0, CYCLES // 256)
    def _(block):
        rows = pl.ds(pl.multiple_of(block * 256, 256), 256)
        out[rows, :] = lax.dot_general(
            colat[rows, :], amps[...], NT, preferred_element_type=F32
        ).astype(BF16)


def forward(pieces, colat, beam, orders, mix):
    return pl.pallas_call(
        forward_kernel,
        in_specs=[in_vmem(), in_vmem(), in_vmem(), in_vmem(), in_smem()],
        out_specs=in_vmem(),
        out_shape=jax.ShapeDtypeStruct((CYCLES, LANES), BF16),
        scratch_shapes=[VMEM((LANES, L), BF16)],
        cost_estimate=pl.CostEstimate(
            flops=2 * CYCLES * L * LANES, bytes_accessed=8_000_000, transcendentals=0
        ),
        name="forward",
    )(pieces, colat, beam, orders, mix)


def partner(value, low):
    return jnp.where(low, pltpu.roll(value, 96, 1), pltpu.roll(value, 32, 1))


def sky_kernel(arrived, azim, noise, mask, turns, out, turned, weighted):
    lane = lax.broadcasted_iota(jnp.int32, (R_DEV, 128), 1)
    left = lane < 64
    low = (lane & 63) < 32

    @pl.loop(0, BLOCKS // 2)
    def _(tile):
        cols = pl.ds(pl.multiple_of(tile * 128, 128), 128)
        sign, cosine, sine = turns[0:1, cols], turns[1:2, cols], turns[2:3, cols]
        for column in range((PAIRS + 1) // 2):
            end = min(column * 128 + 128, LANES)
            first = arrived[2 * tile, :, column * 128 : end].astype(F32)
            second = arrived[2 * tile + 1, :, column * 128 : end].astype(F32)
            if end - column * 128 == 64:
                values = [jnp.concatenate([first, second], axis=1)]
            else:
                values = [
                    jnp.where(left, first, pltpu.roll(second, 64, 1)),
                    jnp.where(left, pltpu.roll(first, 64, 1), second),
                ]
            for offset, value in enumerate(values):
                s, x = divmod(column * 2 + offset, 3)
                straight = cosine * value
                crossed = sine * partner(value, low)
                for q, part in enumerate(
                    (value, straight - crossed, sign * value, straight + crossed)
                ):
                    row = s * 192 + q * 48 + x * R_DEV
                    turned[row : row + R_DEV, cols] = part.astype(BF16)

    @pl.loop(0, QUARTER // 256)
    def _(block):
        start = pl.multiple_of(block * 256, 256)
        cols = pl.ds(start, 256)
        sky = lax.dot_general(turned[...], azim[:, cols], NN, preferred_element_type=F32)
        for q in range(4):
            cells = pl.ds(pl.multiple_of(q * QUARTER + start, 256), 256)
            keep = mask[:, cells].astype(F32)
            for s in range(STOKES):
                for x in range(SLOTS):
                    row = s * 192 + q * 48 + x * R_DEV
                    weight = noise[x, s, :, cells] * keep
                    weighted[row : row + R_DEV, cols] = (
                        weight * sky[row : row + R_DEV, :]
                    ).astype(BF16)

    @pl.loop(0, BLOCKS // 4)
    def _(block):
        rows = pl.ds(pl.multiple_of(block * 256, 256), 256)
        back = lax.dot_general(weighted[...], azim[rows, :], NT, preferred_element_type=F32)
        for sub in range(2):
            tile = block * 2 + sub
            cols = pl.ds(pl.multiple_of(tile * 128, 128), 128)
            sign, cosine, sine = turns[0:1, cols], turns[1:2, cols], turns[2:3, cols]
            lanes = slice(sub * 128, sub * 128 + 128)
            values = []
            for s in range(STOKES):
                for x in range(SLOTS):
                    base = s * 192 + x * R_DEV
                    b0, b1, b2, b3 = (
                        back[base + q * 48 : base + q * 48 + R_DEV, lanes] for q in range(4)
                    )
                    values.append(
                        b0 + sign * b2 + cosine * (b1 + b3) + sine * partner(b1 - b3, low)
                    )
            for column in range(PAIRS // 2):
                even, odd = values[2 * column], values[2 * column + 1]
                span = slice(column * 128, column * 128 + 128)
                out[2 * tile, :, span] = jnp.where(left, even, pltpu.roll(odd, 64, 1)).astype(BF16)
                out[2 * tile + 1, :, span] = jnp.where(left, pltpu.roll(even, 64, 1), odd).astype(
                    BF16
                )
            last = values[-1]
            out[2 * tile, :, LANES - 64 :] = last[:, :64].astype(BF16)
            out[2 * tile + 1, :, LANES - 64 :] = last[:, 64:].astype(BF16)


def sky_pass(arrived, azim, noise, mask, turns):
    return pl.pallas_call(
        sky_kernel,
        in_specs=[in_vmem()] * 5,
        out_specs=in_vmem(),
        out_shape=jax.ShapeDtypeStruct((BLOCKS, R_DEV, LANES), BF16),
        scratch_shapes=[VMEM((4 * PAIRS * R_DEV, 4096), BF16), VMEM((4 * PAIRS * R_DEV, QUARTER), BF16)],
        cost_estimate=pl.CostEstimate(
            flops=2 * 2 * 576 * 4096 * 1024, bytes_accessed=14_000_000, transcendentals=0
        ),
        name="sky",
    )(arrived, azim, noise, mask, turns)


def back_kernel(returned, colat, beam, orders, mix, out, flipped):
    for column in range(LANES // 64):
        lanes = slice(column * 64, column * 64 + 64)
        flipped[lanes, :] = returned[:, lanes].astype(F32).T.astype(BF16)

    @pl.loop(0, L // 256)
    def _(block):
        start = pl.multiple_of(block * 256, 256)
        cols = pl.ds(start, 256)
        harm = lax.dot_general(flipped[...], colat[:, cols], NN, preferred_element_type=F32)
        triangle = at_least(orders[:, 0:1], start, 256)
        piece = block // 2
        inner = pl.ds(pl.multiple_of((block % 2) * 256, 256), 256)
        for s in range(STOKES):
            for k in range(2):
                shaped = []
                for x in range(SLOTS):
                    row = ((s * 3 + x) * 2 + k) * M_DEV
                    shaped.append(harm[row : row + M_DEV, :] * beam[x : x + 1, cols] * triangle)
                for c in range(COMP):
                    total = mix[0, c] * shaped[0]
                    for x in range(1, SLOTS):
                        total = total + mix[x, c] * shaped[x]
                    out[piece, c * 3 + s, k, :, inner] = total.astype(BF16)


def back(returned, colat, beam, orders, mix):
    return pl.pallas_call(
        back_kernel,
        in_specs=[in_vmem(), in_vmem(), in_vmem(), in_vmem(), in_smem()],
        out_specs=in_vmem(),
        out_shape=jax.ShapeDtypeStruct((4, FIELDS, 2, M_DEV, L_DEV), BF16),
        scratch_shapes=[VMEM((LANES, CYCLES), BF16)],
        cost_estimate=pl.CostEstimate(
            flops=2 * CYCLES * L * LANES, bytes_accessed=8_000_000, transcendentals=0
        ),
        name="back",
    )(returned, colat, beam, orders, mix)


def slot_tables(my_slots, mixing, beams):
    select = (my_slots[:, None] == jnp.arange(BANDS, dtype=jnp.int32)[None, :]).astype(F32)
    highest = lax.Precision.HIGHEST
    return (jnp.dot(select, mixing, precision=highest), jnp.dot(select, beams, precision=highest))


def quarter_turns(m_order):
    m_lane = jnp.broadcast_to(m_order.reshape(BLOCKS, 1, M_DEV), (BLOCKS, 2, M_DEV))
    part = jnp.array([1.0, -1.0], F32)[None, :, None]
    phase = m_lane % 4
    sign = jnp.where(phase % 2 == 0, 1.0, -1.0).astype(F32)
    cosine = jnp.where(phase == 0, 1.0, jnp.where(phase == 2, -1.0, 0.0)).astype(F32)
    sine = jnp.where(phase == 1, 1.0, jnp.where(phase == 3, -1.0, 0.0)).astype(F32) * part
    rows = jnp.stack([sign, cosine, sine]).reshape(3, 2 * MODES)
    return jnp.concatenate([rows, jnp.zeros((5, 2 * MODES), F32)])


def on_device(
    solution,
    residual,
    direction,
    precond,
    inv_spec,
    mixing,
    beams,
    slot_band,
    m_order,
    cycle_order,
    inv_noise,
    pix_mask,
):
    band_index = lax.axis_index("band")
    block_index = lax.axis_index(BLK)
    halved = direction.astype(BF16)
    pieces = lax.all_to_all(
        jnp.broadcast_to(halved[None], (4, *halved.shape)), "band", 0, 0, tiled=True
    )
    cycle_mult = jnp.broadcast_to((2 * cycle_order + 1)[:, None], (CYCLES, 128))
    order_mult = jnp.broadcast_to(m_order[:, None], (MODES, 128))
    colat, azim = make_tables(cycle_mult, order_mult)
    turns = quarter_turns(m_order)
    my_orders = lax.dynamic_slice_in_dim(m_order, block_index * M_DEV, M_DEV)
    orders = jnp.broadcast_to(my_orders[:, None], (M_DEV, 128))
    my_slots = lax.dynamic_slice_in_dim(slot_band, band_index * SLOTS, SLOTS)
    slot_mix, slot_beam = slot_tables(my_slots, mixing, beams)
    colat_side = forward(pieces, colat, slot_beam, orders, slot_mix)
    cycle_side = lax.all_to_all(
        colat_side.reshape(BLOCKS, R_DEV, LANES), BLK, split_axis=0, concat_axis=0, tiled=True
    )
    weighted_back = sky_pass(cycle_side, azim, inv_noise, pix_mask, turns)
    returned = lax.all_to_all(weighted_back, BLK, split_axis=0, concat_axis=0, tiled=True)
    combined = back(returned.reshape(CYCLES, LANES), colat, slot_beam, orders, slot_mix)
    parts = lax.all_to_all(combined, "band", 0, 0, tiled=True)
    data_term = jnp.sum(parts.astype(F32), axis=0)
    prior_diag = inv_spec[:, None, None, :]
    precond_full = precond[:, None, None, :]
    applied = prior_diag * direction + data_term
    scaled_res = precond_full * residual
    sums = jnp.stack(
        [
            jnp.sum(residual * scaled_res),
            jnp.sum(direction * applied),
            jnp.sum(applied * scaled_res),
            jnp.sum(applied * precond_full * applied),
        ]
    )
    norm_old, curvature, crossed, squared = lax.psum(sums, BAND_BLK)
    step_size = norm_old / curvature
    solution_next = solution + step_size * direction
    residual_next = residual - step_size * applied
    scaled_next = precond_full * residual_next
    norm_new = norm_old - 2.0 * step_size * crossed + step_size * step_size * squared
    direction_next = scaled_next + norm_new / norm_old * direction
    return (solution_next, residual_next, direction_next)


def solution(mesh):
    finer = Mesh(
        mesh.devices.reshape(mesh.shape["band"], 8, 4, 2), ("band", "blk_0", "blk_1", "blk_2")
    )
    in_specs = (
        P(None, None, BLK, "band"),
        P(None, None, BLK, "band"),
        P(None, None, BLK, "band"),
        P(None, "band"),
        P(None, "band"),
        P(),
        P(),
        P(),
        P(),
        P(),
        P("band", None, BLK, None),
        P(BLK, None),
    )
    out_specs = (P(None, None, BLK, "band"), P(None, None, BLK, "band"), P(None, None, BLK, "band"))
    return jax.shard_map(
        on_device, mesh=finer, in_specs=in_specs, out_specs=out_specs, check_vma=False
    )
```

time: 468 us -> 295 us (0.63)
  local copies, waits for them, and re-layouts: 119 us -> 8.9 us
  matrix products: 106 us -> 1.61 us
  other arithmetic: 74.2 us -> 11.3 us
  Pallas kernels: 0 us -> 57.3 us
  blocking collectives: 113 us -> 147 us
  waiting for transfers between devices: 26.5 us -> 44.3 us
    dot_general x10 -> x0, matrix products: 106 us -> none  [the longest x1 48.8 us: combine_bands(): jnp.einsum('sxrkm,rl->sxkml', returned, colat, preferred_element_type=jnp...]
    pallas_call x0 -> x4, Pallas kernels: none -> 57.3 us  [the longest x1 27.5 us: sky_pass(): pl.pallas_call(sky_kernel, in_specs=[in_vmem()] * 5, out_specs=in_vmem(),...]
    unnamed x51 -> x24, local copies, waits for them, and re-layouts: 51.8 us -> 2.94 us
    another operation x3 -> x2, other arithmetic: 42.5 us -> 3.26 us  [the longest x1 2.54 us: on_device(): jnp.stack([jnp.sum(residual * scaled_res), jnp.sum(direction * applied),...]
    all_to_all x4 -> x0, local copies, waits for them, and re-layouts: 34.7 us -> none  [the longest x1 20.3 us: on_device(): lax.all_to_all(weighted_back, BLK, split_axis=4, concat_axis=2, tiled=True)]
    psum x4 -> x1, blocking collectives: 42.2 us -> 75.3 us  [on_device(): norm_old, curvature, crossed, squared = lax.psum(sums, BAND_BLK)]
    convert_element_type x3 -> x0, local copies, waits for them, and re-layouts: 28.3 us -> none  [the longest x1 16.8 us: sky_weights(): return running.astype(jnp.bfloat16)]
    all_to_all x2, waiting for transfers between devices: 26.5 us -> 44.3 us  [the longest x1 32.3 us: on_device(): lax.all_to_all(colat_side.reshape(BLOCKS, R_DEV, LANES), BLK, split_axis=...]
  transfers between devices with their start and end apart: 2 -> 2, of which waited for: 1 -> 2; matrix products, arithmetic and copies ran while one was open for 10% -> 2% of each run, Pallas kernels for 0% -> 4%
where the time goes in v1:
time: 295 us; the launch traced here: 294 us
  blocking collectives  147 us (50%)
  Pallas kernels  57.3 us (19%)
  waiting for transfers between devices  44.3 us (15%)
  starting transfers between devices  19.6 us (7%)
  other arithmetic  11.3 us (4%)
  local copies, waits for them, and re-layouts  8.9 us (3%)
  between operations  4.41 us (1%)
    psum x1, blocking collectives, on_device(): norm_old, curvature, crossed, squared = lax.psum(sums, BAND_BLK)  75.3 us
    all_to_all x1, blocking collectives, on_device(): lax.all_to_all(weighted_back, BLK, split_axis=0, concat_axis=0, tiled=True)  40.1 us
    all_to_all x1, waiting for transfers between devices, on_device(): lax.all_to_all(colat_side.reshape(BLOCKS, R_DEV, LANES), BLK, split_axis=...  32.3 us
    all_to_all x1, blocking collectives, on_device(): parts = lax.all_to_all(combined, 'band', 0, 0, tiled=True)  31.2 us
    pallas_call x1, Pallas kernels, sky_pass(): pl.pallas_call(sky_kernel, in_specs=[in_vmem()] * 5, out_specs=in_vmem(),...  27.5 us
    all_to_all x1, starting transfers between devices, on_device(): lax.all_to_all(colat_side.reshape(BLOCKS, R_DEV, LANES), BLK, split_axis=...  14.6 us
    all_to_all x1, waiting for transfers between devices, on_device(): lax.all_to_all(jnp.broadcast_to(halved[None], (4, *halved.shape)), 'band'...  12 us
    pallas_call x1, Pallas kernels, make_tables(): pl.pallas_call(tables_kernel, grid=(steps,), in_specs=[pl.BlockSpec((CYCL...  11.2 us
  transfers between devices with their start and end apart: 2, of which 2 were waited for; matrix products, arithmetic and copies ran while one was open for 2% of the time, Pallas kernels for 4%

profile of v1, /device:TPU:1, one launch (start us, length us, event | category | flops | bytes accessed | tf_op | source)
XLA Modules:
  0.0 293.9 jit_solution(17576563813671225996)
XLA Ops:
  0.6 1.4 convert_element_type.7
  2.0 1.7 broadcast_in_dim.58
  3.8 5.0 %all-to-all-start = ((bf16[4,9,2,32,512]{4,3,2,1,0:T(8,128)(2,1)}), bf16[4,9,2,32,512]{4,3,2,1,0:T(8,128)(2,1)S(1)}, u32[]{:S(2)}, u32[]{:S(2)}) async-start(bf16[4,9,2,32,512]{4,3,2,1,0:T(8,128)(2,1)} %broadcast_in_dim.58), calls=%async_computation | async-start | bytes 4718592 | tf_op jit(solution)/shard_map/all_to_all | solution.py:348
  8.9 1.0 broadcast_in_dim.59.cycle_mult
  9.9 1.3 broadcast_in_dim.60.order_mult
  11.2 11.2 %tables.1 = (bf16[1024,2048]{1,0:T(8,128)(2,1)}, bf16[4096,1024]{1,0:T(8,128)(2,1)}) custom-call(s32[1024,128]{1,0:T(8,128)} %broadcast_in_dim.59.cycle_mult, s32[2048,128]{1,0:T(8,128)} %broadcast_in_dim.60.order_mult), custom_call_target="tpu_custom_call" | custom-call | flops 60000000 | bytes 14000000 | tf_op jit(solution)/shard_map/tables/pallas_call | solution.py:111
  22.4 0.8 fusion.6.mix
  23.2 0.8 fusion.7.beam
  24.0 12.0 %all-to-all-done.pieces = bf16[4,9,2,32,512]{4,3,2,1,0:T(8,128)(2,1)S(1)} async-done(((bf16[4,9,2,32,512]{4,3,2,1,0:T(8,128)(2,1)}), bf16[4,9,2,32,512]{4,3,2,1,0:T(8,128)(2,1)S(1)}, u32[]{:S(2)}, u32[]{:S(2)}) %all-to-all-start) | async-done | bytes 2359328 | tf_op jit(solution)/shard_map/all_to_all | solution.py:348
  36.0 0.8 broadcast_in_dim.61.orders
  37.4 9.4 %forward.1 = bf16[1024,576]{1,0:T(8,128)(2,1)} custom-call(bf16[4,9,2,32,512]{4,3,2,1,0:T(8,128)(2,1)} %copy-done.3, bf16[1024,2048]{1,0:T(8,128)(2,1)} %get-tuple-element.5.colat, f32[3,2048]{1,0:T(4,128)} %fusion.7.beam, s32[32,128]{1,0:T(8,128)} %broadcast_in_dim.61.orders, f32[3,3]{1,0:T(4,128)} %fusion.6.mix), custom_call_target="tpu_custom_call" | custom-call | flops 2415919104 | bytes 8000000 | tf_op jit(solution)/shard_map/forward/pallas_call | solution.py:166
  46.9 14.6 %all-to-all-start.1 = ((bf16[64,16,576]{2,1,0:T(8,128)(2,1)}), bf16[64,16,576]{2,1,0:T(8,128)(2,1)S(1)}, u32[]{:S(2)}, u32[]{:S(2)}) async-start(bf16[64,16,576]{2,1,0:T(8,128)(2,1)} %bitcast.12), calls=%async_computation.1 | async-start | bytes 2621440 | tf_op jit(solution)/shard_map/all_to_all | solution.py:360
  62.1 0.7 select_maximum_fusion.turns
  62.9 32.3 %all-to-all-done.1.arrived = bf16[64,16,576]{2,1,0:T(8,128)(2,1)S(1)} async-done(((bf16[64,16,576]{2,1,0:T(8,128)(2,1)}), bf16[64,16,576]{2,1,0:T(8,128)(2,1)S(1)}, u32[]{:S(2)}, u32[]{:S(2)}) %all-to-all-start.1) | async-done | bytes 1179680 | tf_op jit(solution)/shard_map/all_to_all | solution.py:360
  95.1 1.1 copy-done.4
  96.2 27.5 %sky.1 = bf16[64,16,576]{2,1,0:T(8,128)(2,1)} custom-call(bf16[64,16,576]{2,1,0:T(8,128)(2,1)} %copy-done.4, bf16[4096,1024]{1,0:T(8,128)(2,1)} %get-tuple-element.6.azim, f32[3,3,16,4096]{3,2,1,0:T(8,128)} %noise.1, s32[16,4096]{1,0:T(8,128)} %mask.1, f32[8,4096]{1,0:T(8,128)} %select_maximum_fusion.turns), custom_call_target="tpu_custom_call" | custom-call | flops 9663676416 | bytes 14000000 | tf_op jit(solution)/shard_map/sky/pallas_call | solution.py:261
  123.7 40.1 %all_to_all.20 = bf16[64,16,576]{2,1,0:T(8,128)(2,1)} all-to-all(bf16[64,16,576]{2,1,0:T(8,128)(2,1)} %sky.1), channel_id=1, replica_groups=mesh['band'=4,'blk_0'=8,'blk_1'=4,'blk_2'=2] {'blk_0','blk_1','blk_2'}, dimensions={0} | all-to-all | bytes 2359296 | tf_op jit(solution)/shard_map/all_to_all | solution.py:364
  163.8 9.1 %back.1 = bf16[4,9,2,32,512]{4,3,2,1,0:T(8,128)(2,1)} custom-call(bf16[1024,576]{1,0:T(8,128)(2,1)} %bitcast.13, bf16[1024,2048]{1,0:T(8,128)(2,1)} %get-tuple-element.5.colat, f32[3,2048]{1,0:T(4,128)} %fusion.7.beam, s32[32,128]{1,0:T(8,128)} %broadcast_in_dim.61.orders, f32[3,3]{1,0:T(4,128)} %fusion.6.mix), custom_call_target="tpu_custom_call" | custom-call | flops 2415919104 | bytes 8000000 | tf_op jit(solution)/shard_map/back/pallas_call | solution.py:301
  172.9 31.2 %all_to_all.21 = bf16[4,9,2,32,512]{4,3,2,1,0:T(8,128)(2,1)S(1)} all-to-all(bf16[4,9,2,32,512]{4,3,2,1,0:T(8,128)(2,1)} %back.1), channel_id=1, replica_groups=mesh['band'=4,'blk_0'=8,'blk_1'=4,'blk_2'=2] {'band'}, dimensions={0} | all-to-all | bytes 4718592 | tf_op jit(solution)/shard_map/all_to_all | solution.py:366
  204.6 0.8 copy-done.1
  205.8 2.1 fusion
  207.9 2.5 pad_maximum_fusion
  210.5 75.3 %psum.7 = f32[4]{0:T(128)S(1)} all-reduce(f32[4]{0:T(128)S(1)} %pad_maximum_fusion), channel_id=1, replica_groups=mesh['band'=4,'blk_0'=8,'blk_1'=4,'blk_2'=2] {'band','blk_0','blk_1','bl..., use_global_device_ids=true, to_apply=%region_5.6 | all-reduce | flops 4 | bytes 32 | tf_op jit(solution)/shard_map/psum | solution.py:380
  290.0 3.9 %multiply_add_fusion = (f32[9,2,32,512]{3,2,1,0:T(8,128)}, f32[9,2,32,512]{3,2,1,0:T(8,128)}, f32[9,2,32,512]{3,2,1,0:T(8,128)}) fusion(f32[9,2,32,512]{3,2,1,0:T(8,128)S(1)} %copy-done.1, f32[]{:T(128)S(6)} %div.7, f32[9,512]{1,0:T(8,128)S(1)} %copy-done.5, f32[9,2,32,512]{3,2,1,0:T(8,128)S(1)} %copy-done.2, f32[9,2,32,512]{3,2,1,0:T(8,128)} %get-tuple-element.13, ...), kind=kLoop, calls=%fused_computation.7 | loop fusion | flops 2064384 | bytes 8275976 | tf_op jit(solution)/shard_map/add | solution.py:386
  (35 shorter events, 2.8 us)
Async XLA Ops:
  0.6 22.5 %copy-start = (f32[9,2048]{1,0:T(8,128)S(1)}, f32[9,2048]{1,0:T(8,128)}, u32[]{:S(2)}) copy-start(f32[9,2048]{1,0:T(8,128)} %param.19) | copy-start | bytes 221188
  3.8 5.0 %copy-start.11 = (s32[12]{0:T(128)S(1)}, s32[12]{0:T(128)}, u32[]{:S(2)}) copy-start(s32[12]{0:T(128)} %param.20) | copy-start | bytes 148
  3.8 5.0 %copy-start.7 = (s32[2048]{0:T(1024)S(1)}, s32[2048]{0:T(1024)}, u32[]{:S(2)}) copy-start(s32[2048]{0:T(1024)} %param.21) | copy-start | bytes 24580
  3.8 5.1 %copy-start.8 = (s32[1024]{0:T(1024)S(1)}, s32[1024]{0:T(1024)}, u32[]{:S(2)}) copy-start(s32[1024]{0:T(1024)} %param.22) | copy-start | bytes 12292
  3.8 32.2 %all-to-all-start = ((bf16[4,9,2,32,512]{4,3,2,1,0:T(8,128)(2,1)}), bf16[4,9,2,32,512]{4,3,2,1,0:T(8,128)(2,1)S(1)}, u32[]{:S(2)}, u32[]{:S(2)}) async-start(bf16[4,9,2,32,512]{4,3,2,1,0:T(8,128)(2,1)} %broadcast_in_dim.58), calls=%async_computation | async-start | bytes 4718592 | tf_op jit(solution)/shard_map/all_to_all | solution.py:348
  9.9 12.5 %copy-start.10 = (f32[9,3]{0,1:T(4,128)S(1)}, f32[9,3]{0,1:T(4,128)}, u32[]{:S(2)}) copy-start(f32[9,3]{0,1:T(4,128)} %param.18) | copy-start | bytes 328
  36.0 1.4 copy-start.3
  46.9 14.9 %copy-start.9 = (f32[2]{0:T(128)S(1)}, f32[2]{0:T(128)}, u32[]{:S(2)}) copy-start(f32[2]{0:T(128)} %constant.69.clone) | copy-start | bytes 28
  46.9 48.2 %all-to-all-start.1 = ((bf16[64,16,576]{2,1,0:T(8,128)(2,1)}), bf16[64,16,576]{2,1,0:T(8,128)(2,1)S(1)}, u32[]{:S(2)}, u32[]{:S(2)}) async-start(bf16[64,16,576]{2,1,0:T(8,128)(2,1)} %bitcast.12), calls=%async_computation.1 | async-start | bytes 2621440 | tf_op jit(solution)/shard_map/all_to_all | solution.py:360
  95.1 1.1 copy-start.4
  204.2 1.3 copy-start.1
  204.2 1.6 copy-start.2
  204.2 1.6 copy-start.5
  204.2 1.6 copy-start.6

commit v2 on v1

v2 whole, which is shorter than its diff:
```python
import math

import jax
import jax.numpy as jnp
from jax import lax
from jax.experimental import pallas as pl
from jax.experimental.pallas import tpu as pltpu
from jax.sharding import Mesh
from jax.sharding import PartitionSpec as P

COMP = 3
STOKES = 3
FIELDS = 9
BANDS = 9
SLOTS = 3
L = 2048
CYCLES = 1024
MODES = 2048
PHI = 4096
QUARTER = PHI // 4
M_DEV = 32
R_DEV = 16
BLOCKS = 64
L_DEV = 512
BLK = ("blk_0", "blk_1", "blk_2")
SCALE = 1.0 / math.sqrt(2048)
VMEM = pltpu.VMEM
MESH = pl.DeviceIdType.MESH
F32 = jnp.float32
BF16 = jnp.bfloat16
NT = (((1,), (1,)), ((), ()))
NN = (((1,), (0,)), ((), ()))


def in_vmem():
    return pl.BlockSpec(memory_space=VMEM)


def in_smem():
    return pl.BlockSpec(memory_space=pltpu.SMEM)


def unit_circle(turn):
    half = (((turn + 2048) & 4095) - 2048).astype(F32) * (math.pi / 4096)
    sq = half * half
    sine = half * (
        1
        + sq
        * (-1 / 6 + sq * (1 / 120 + sq * (-1 / 5040 + sq * (1 / 362880 + sq * (-1 / 39916800)))))
    )
    cosine = 1 + sq * (
        -1 / 2
        + sq
        * (
            1 / 24
            + sq * (-1 / 720 + sq * (1 / 40320 + sq * (-1 / 3628800 + sq * (1 / 479001600))))
        )
    )
    return cosine * cosine - sine * sine, 2 * sine * cosine


def first_turns(mult):
    lane = lax.broadcasted_iota(jnp.int32, mult.shape, 1)
    cosine, sine = unit_circle((mult * lane) & 4095)
    step_cos, step_sin = unit_circle((mult * 128) & 4095)
    return cosine * SCALE, sine * SCALE, step_cos, step_sin


def colat_rows(mult, store):
    cosine, sine, step_cos, step_sin = first_turns(mult)
    for tile in range(L // 128):
        store(tile, cosine.astype(BF16))
        cosine, sine = cosine * step_cos - sine * step_sin, sine * step_cos + cosine * step_sin


def azim_rows(mult, store):
    cosine, sine, step_cos, step_sin = first_turns(mult)
    for tile in range(QUARTER // 128):
        store(tile, cosine.astype(BF16), (-sine).astype(BF16))
        cosine, sine = cosine * step_cos - sine * step_sin, sine * step_cos + cosine * step_sin


def at_least(orders, first, width):
    l_values = first + lax.broadcasted_iota(jnp.int32, (M_DEV, width), 1)
    return (l_values >= orders).astype(F32)


def partner(value, low):
    return jnp.where(low, pltpu.roll(value, 96, 1), pltpu.roll(value, 32, 1))


def folded(value):
    tiles = [
        value[8 * i : 8 * i + 8, 128 * j : 128 * j + 128]
        for i in range(value.shape[0] // 8)
        for j in range(value.shape[1] // 128)
    ]
    while len(tiles) > 1:
        tiles = [first + second for first, second in zip(tiles[::2], tiles[1::2])]
    return tiles[0]


def operator_kernel(
    direction_in,
    residual_in,
    noise_in,
    mask_in,
    cycle_mult,
    order_mult,
    turns,
    orders,
    beam,
    precond,
    inv_spec,
    mix,
    applied,
    sums,
    direction,
    residual,
    noise,
    mask,
    gathered,
    colat,
    azim,
    amps,
    there,
    there_mid,
    arrived,
    turned,
    weighted,
    home,
    home_mid,
    returned,
    flipped,
    combined,
    parts,
    totals,
    sum_y,
    sum_z,
    sum_x,
    load_sem,
    gather_send,
    gather_recv,
    z_send,
    z_recv,
    y_send,
    y_recv,
    x_send,
    x_recv,
    sum_send,
    sum_recv,
):
    x_me = lax.axis_index("band")
    z_me = lax.axis_index("blk_0")
    y_me = lax.axis_index("blk_1") * 2 + lax.axis_index("blk_2")
    right, left, across = (lax.rem(x_me + off, 4) for off in (1, 3, 2))
    z_others = [lax.rem(z_me + off, 8) for off in range(1, 8)]
    y_others = [lax.rem(y_me + off, 8) for off in range(1, 8)]

    def at_x(index):
        return {"band": index}

    def at_z(index):
        return {"blk_0": index}

    def at_y(index):
        return {"blk_1": lax.div(index, 2), "blk_2": lax.rem(index, 2)}

    peers = [at_x(i) for i in (right, left, across)]
    peers += [at_z(i) for i in z_others] + [at_y(i) for i in y_others]
    barrier = pltpu.get_barrier_semaphore()
    for peer in peers:
        pl.semaphore_signal(barrier, inc=1, device_id=peer, device_id_type=MESH)

    loads = [
        pltpu.make_async_copy(source, target, load_sem.at[index])
        for index, (source, target) in enumerate(
            ((direction_in, direction), (mask_in, mask), (noise_in, noise), (residual_in, residual))
        )
    ]
    for load in loads:
        load.start()

    sent = []

    def send(source, target, send_sem, recv_sem, peer):
        copy = pltpu.make_async_remote_copy(
            src_ref=source,
            dst_ref=target,
            send_sem=send_sem,
            recv_sem=recv_sem,
            device_id=peer,
            device_id_type=MESH,
        )
        copy.start()
        sent.append(copy)
        return copy

    def arrive(copies):
        for copy in copies:
            copy.wait_recv()

    loads[0].wait()
    for s in range(STOKES):
        for k in range(2):
            for c in range(COMP):
                gathered[s, x_me, k, c] = direction[c * 3 + s, k].astype(BF16)
        if s == 0:
            pl.semaphore_wait(barrier, len(peers))
        if s == 0:
            direct = []
        direct.append(
            [
                send(
                    gathered.at[s, x_me],
                    gathered.at[s, x_me],
                    gather_send.at[s, way],
                    gather_recv.at[s, way],
                    at_x(peer),
                )
                for way, peer in enumerate((right, left))
            ]
        )

    def forward_on(s):
        arrive(direct[s])
        return [
            send(
                gathered.at[s, source, way],
                gathered.at[s, source, way],
                gather_send.at[s, 2 + way],
                gather_recv.at[s, 2 + way],
                at_x(peer),
            )
            for way, (source, peer) in enumerate(((left, right), (right, left)))
        ]

    def make_colat():
        @pl.loop(0, CYCLES // 32)
        def _(block):
            rows = pl.ds(pl.multiple_of(block * 32, 32), 32)

            def put(tile, value):
                colat[rows, tile * 128 : (tile + 1) * 128] = value

            colat_rows(cycle_mult[rows, :], put)

    def make_azim():
        @pl.loop(0, BLOCKS)
        def _(block):
            rows = pl.ds(pl.multiple_of(block * 32, 32), 32)
            real_rows = pl.ds(pl.multiple_of(block * 64, 32), 32)
            imag_rows = pl.ds(pl.multiple_of(block * 64 + 32, 32), 32)

            def put(tile, real, imag):
                azim[real_rows, tile * 128 : (tile + 1) * 128] = real
                azim[imag_rows, tile * 128 : (tile + 1) * 128] = imag

            azim_rows(order_mult[rows, :], put)

    lane = lax.broadcasted_iota(jnp.int32, (R_DEV, 128), 1)
    on_left = lane < 64
    on_left8 = on_left[:8]
    low = (lane & 63) < 32

    def legendre(s):
        @pl.loop(0, L // 256)
        def _(block):
            first = pl.multiple_of(block * 256, 256)
            piece = block // 2
            inner = pl.ds(pl.multiple_of((block % 2) * 256, 256), 256)
            triangle = at_least(orders[:, 0:1], first, 256)
            for k in range(2):
                comps = [gathered[s, piece, k, c, :, inner].astype(F32) for c in range(COMP)]
                for x in range(SLOTS):
                    mixed = mix[x, 0] * comps[0]
                    for c in range(1, COMP):
                        mixed = mixed + mix[x, c] * comps[c]
                    row = (x * 2 + k) * M_DEV
                    value = mixed * beam[x : x + 1, pl.ds(first, 256)] * triangle
                    amps[row : row + M_DEV, pl.ds(first, 256)] = value.astype(BF16)

        @pl.loop(0, CYCLES // 256)
        def _(block):
            rows = pl.ds(pl.multiple_of(block * 256, 256), 256)
            side = lax.dot_general(colat[rows, :], amps[...], NT, preferred_element_type=F32)
            main = side[:, :128].reshape(2, 8, 16, 128)
            tail = side[:, 128:].reshape(16, 16, 128)
            wide = lax.broadcasted_iota(jnp.int32, (128, 128), 1) < 64
            packed = jnp.where(
                wide,
                tail[:, :8].reshape(128, 128),
                pltpu.roll(tail[:, 8:].reshape(128, 128), 64, 1),
            )
            there[s, pl.ds(block * 2, 2), :, 0:16, :] = main.astype(BF16)
            there[s, pl.ds(block * 2, 2), :, 16:24, :] = packed.reshape(2, 8, 8, 128).astype(BF16)

    def start_z(way, s, source, middle):
        copies = [
            send(
                source.at[s, other],
                middle.at[s, z_me],
                z_send.at[way, s, index],
                z_recv.at[way, s, index],
                at_z(other),
            )
            for index, other in enumerate(z_others)
        ]
        middle[s, z_me] = source[s, z_me]
        return copies

    def start_y(way, s, middle, target):
        copies = [
            send(
                middle.at[s, :, other],
                target.at[s, :, y_me],
                y_send.at[way, s, index],
                y_recv.at[way, s, index],
                at_y(other),
            )
            for index, other in enumerate(y_others)
        ]
        target[s, :, y_me] = middle[s, :, y_me]
        return copies

    def azimuth(s):
        @pl.loop(0, BLOCKS // 2)
        def _(tile):
            cols = pl.ds(pl.multiple_of(tile * 128, 128), 128)
            sign, cosine, sine = turns[0:1, cols], turns[1:2, cols], turns[2:3, cols]
            plane, place = tile // 4, (tile % 4) * 2
            first = arrived[s, plane, place, 0:16, :].astype(F32)
            second = arrived[s, plane, place + 1, 0:16, :].astype(F32)
            third = arrived[s, plane, place, 16:24, :].astype(F32)
            fourth = arrived[s, plane, place + 1, 16:24, :].astype(F32)
            values = [
                jnp.where(on_left, first, pltpu.roll(second, 64, 1)),
                jnp.where(on_left, pltpu.roll(first, 64, 1), second),
                jnp.concatenate(
                    [
                        jnp.where(on_left8, third, pltpu.roll(fourth, 64, 1)),
                        jnp.where(on_left8, pltpu.roll(third, 64, 1), fourth),
                    ],
                    axis=0,
                ),
            ]
            for x, value in enumerate(values):
                straight = cosine * value
                crossed = sine * partner(value, low)
                for q, part in enumerate(
                    (value, straight - crossed, sign * value, straight + crossed)
                ):
                    row = q * 48 + x * R_DEV
                    turned[row : row + R_DEV, cols] = part.astype(BF16)

        @pl.loop(0, QUARTER // 256)
        def _(block):
            start = pl.multiple_of(block * 256, 256)
            cols = pl.ds(start, 256)
            sky = lax.dot_general(turned[...], azim[:, cols], NN, preferred_element_type=F32)
            for q in range(4):
                cells = pl.ds(pl.multiple_of(q * QUARTER + start, 256), 256)
                keep = mask[:, cells].astype(F32)
                for x in range(SLOTS):
                    row = q * 48 + x * R_DEV
                    weight = noise[x, s, :, cells] * keep
                    weighted[row : row + R_DEV, cols] = (
                        weight * sky[row : row + R_DEV, :]
                    ).astype(BF16)

        @pl.loop(0, BLOCKS // 4)
        def _(block):
            rows = pl.ds(pl.multiple_of(block * 256, 256), 256)
            back = lax.dot_general(weighted[...], azim[rows, :], NT, preferred_element_type=F32)
            for sub in range(2):
                tile = block * 2 + sub
                cols = pl.ds(pl.multiple_of(tile * 128, 128), 128)
                sign, cosine, sine = turns[0:1, cols], turns[1:2, cols], turns[2:3, cols]
                lanes = slice(sub * 128, sub * 128 + 128)
                values = []
                for x in range(SLOTS):
                    b0, b1, b2, b3 = (
                        back[q * 48 + x * R_DEV : q * 48 + x * R_DEV + R_DEV, lanes]
                        for q in range(4)
                    )
                    values.append(
                        b0 + sign * b2 + cosine * (b1 + b3) + sine * partner(b1 - b3, low)
                    )
                zero, one, two = values
                plane, place = tile // 4, (tile % 4) * 2
                home[s, plane, place, 0:16, :] = jnp.where(
                    on_left, zero, pltpu.roll(one, 64, 1)
                ).astype(BF16)
                home[s, plane, place + 1, 0:16, :] = jnp.where(
                    on_left, pltpu.roll(zero, 64, 1), one
                ).astype(BF16)
                home[s, plane, place, 16:24, :] = jnp.where(
                    on_left8, two[:8], pltpu.roll(two[8:], 64, 1)
                ).astype(BF16)
                home[s, plane, place + 1, 16:24, :] = jnp.where(
                    on_left8, pltpu.roll(two[:8], 64, 1), two[8:]
                ).astype(BF16)

    def legendre_back(s):
        @pl.loop(0, 8)
        def _(plane):
            cols = pl.ds(pl.multiple_of(plane * 128, 128), 128)
            main = returned[s, plane, :, 0:16, :].astype(F32).reshape(128, 128)
            tail = returned[s, plane, :, 16:24, :].astype(F32)
            swapped = pltpu.roll(tail.reshape(64, 128), 64, 1).reshape(8, 8, 128)
            both = jnp.concatenate([tail, swapped], axis=1).reshape(128, 128)
            flipped[0:128, cols] = main.T.astype(BF16)
            flipped[128:256, cols] = both.T.astype(BF16)

        @pl.loop(0, L // 256)
        def _(block):
            start = pl.multiple_of(block * 256, 256)
            cols = pl.ds(start, 256)
            harm = lax.dot_general(
                flipped[0:192, :], colat[:, cols], NN, preferred_element_type=F32
            )
            triangle = at_least(orders[:, 0:1], start, 256)
            piece = block // 2
            inner = pl.ds(pl.multiple_of((block % 2) * 256, 256), 256)
            for k in range(2):
                shaped = []
                for x in range(SLOTS):
                    row = (x * 2 + k) * M_DEV
                    shaped.append(harm[row : row + M_DEV, :] * beam[x : x + 1, cols] * triangle)
                for c in range(COMP):
                    total = mix[0, c] * shaped[0]
                    for x in range(1, SLOTS):
                        total = total + mix[x, c] * shaped[x]
                    combined[s, piece, c, k, :, inner] = total.astype(BF16)

    def start_x(s):
        return [
            send(
                combined.at[s, other],
                parts.at[s, index],
                x_send.at[s, index],
                x_recv.at[s, index],
                at_x(other),
            )
            for index, other in enumerate((right, left, across))
        ]

    def apply(s):
        for c in range(COMP):
            field = c * 3 + s
            pre = precond[field : field + 1, :]
            prior = inv_spec[field : field + 1, :]
            for k in range(2):
                total = combined[s, x_me, c, k].astype(F32)
                for index in range(3):
                    total = total + parts[s, index, c, k].astype(F32)
                dir_now = direction[field, k]
                res_now = residual[field, k]
                value = prior * dir_now + total
                applied[field, k] = value
                scaled = pre * res_now
                totals[0] += folded(res_now * scaled)
                totals[1] += folded(dir_now * value)
                totals[2] += folded(value * scaled)
                totals[3] += folded(value * pre * value)

    def sum_over(stage, buffer, me, others, place, value):
        buffer[me] = value
        copies = [
            send(
                buffer.at[me],
                buffer.at[me],
                sum_send.at[stage, index],
                sum_recv.at[stage, index],
                place(other),
            )
            for index, other in enumerate(others)
        ]
        arrive(copies)
        return jnp.sum(buffer[...], axis=0)

    totals[...] = jnp.zeros_like(totals)
    amps[192:256, :] = jnp.zeros((64, L), BF16)
    make_colat()
    relayed = [forward_on(0)]
    for load in loads[1:]:
        load.wait()
    arrive(relayed[0])
    legendre(0)
    z_there = [start_z(0, 0, there, there_mid)]
    relayed.append(forward_on(1))
    make_azim()
    relayed.append(forward_on(2))
    arrive(relayed[1])
    legendre(1)
    z_there.append(start_z(0, 1, there, there_mid))
    arrive(z_there[0])
    y_there = [start_y(0, 0, there_mid, arrived)]
    arrive(relayed[2])
    legendre(2)
    z_there.append(start_z(0, 2, there, there_mid))
    arrive(y_there[0])
    azimuth(0)
    z_home = [start_z(1, 0, home, home_mid)]
    arrive(z_there[1])
    y_there.append(start_y(0, 1, there_mid, arrived))
    arrive(y_there[1])
    azimuth(1)
    z_home.append(start_z(1, 1, home, home_mid))
    arrive(z_there[2])
    y_there.append(start_y(0, 2, there_mid, arrived))
    arrive(y_there[2])
    azimuth(2)
    z_home.append(start_z(1, 2, home, home_mid))
    arrive(z_home[0])
    y_home = [start_y(1, 0, home_mid, returned)]
    arrive(y_home[0])
    legendre_back(0)
    x_home = [start_x(0)]
    arrive(z_home[1])
    y_home.append(start_y(1, 1, home_mid, returned))
    arrive(y_home[1])
    legendre_back(1)
    x_home.append(start_x(1))
    arrive(z_home[2])
    y_home.append(start_y(1, 2, home_mid, returned))
    arrive(x_home[0])
    apply(0)
    arrive(y_home[2])
    legendre_back(2)
    x_home.append(start_x(2))
    arrive(x_home[1])
    apply(1)
    arrive(x_home[2])
    apply(2)

    row = lax.broadcasted_iota(jnp.int32, (8, 128), 0)
    value = jnp.zeros((8, 128), F32)
    for index in range(4):
        value = jnp.where(row == index, jnp.sum(totals[index], axis=0, keepdims=True), value)
    value = sum_over(0, sum_y, y_me, y_others, at_y, value)
    value = sum_over(1, sum_z, z_me, z_others, at_z, value)
    value = sum_over(2, sum_x, x_me, (right, left, across), at_x, value)
    sums[...] = jnp.broadcast_to(jnp.sum(value, axis=1, keepdims=True), (8, 128))
    for copy in sent:
        copy.wait_send()


def operator(direction, residual, noise, mask, *small):
    dma = pltpu.SemaphoreType.DMA
    block = (STOKES, 8, 8, 24, 128)
    local = (FIELDS, 2, M_DEV, L_DEV)
    return pl.pallas_call(
        operator_kernel,
        in_specs=[pl.BlockSpec(memory_space=pl.ANY)] * 4 + [in_vmem()] * 7 + [in_smem()],
        out_specs=[in_vmem(), in_vmem()],
        out_shape=[jax.ShapeDtypeStruct(local, F32), jax.ShapeDtypeStruct((8, 128), F32)],
        scratch_shapes=[
            VMEM(local, F32),
            VMEM(local, F32),
            VMEM((SLOTS, STOKES, R_DEV, PHI), F32),
            VMEM((R_DEV, PHI), jnp.int32),
            VMEM((STOKES, 4, 2, COMP, M_DEV, L_DEV), BF16),
            VMEM((CYCLES, L), BF16),
            VMEM((2 * MODES, QUARTER), BF16),
            VMEM((256, L), BF16),
            VMEM(block, BF16),
            VMEM(block, BF16),
            VMEM(block, BF16),
            VMEM((192, 2 * MODES), BF16),
            VMEM((192, QUARTER), BF16),
            VMEM(block, BF16),
            VMEM(block, BF16),
            VMEM(block, BF16),
            VMEM((256, CYCLES), BF16),
            VMEM((STOKES, 4, COMP, 2, M_DEV, L_DEV), BF16),
            VMEM((STOKES, 3, COMP, 2, M_DEV, L_DEV), BF16),
            VMEM((4, 8, 128), F32),
            VMEM((8, 8, 128), F32),
            VMEM((8, 8, 128), F32),
            VMEM((4, 8, 128), F32),
            dma((4,)),
            dma((STOKES, 4)),
            dma((STOKES, 4)),
            dma((2, STOKES, 7)),
            dma((2, STOKES, 7)),
            dma((2, STOKES, 7)),
            dma((2, STOKES, 7)),
            dma((STOKES, 3)),
            dma((STOKES, 3)),
            dma((3, 7)),
            dma((3, 7)),
        ],
        compiler_params=pltpu.CompilerParams(
            collective_id=0, has_side_effects=True, vmem_limit_bytes=60 * 1024 * 1024
        ),
        name="operator",
    )(direction, residual, noise, mask, *small)


def slot_tables(my_slots, mixing, beams):
    select = (my_slots[:, None] == jnp.arange(BANDS, dtype=jnp.int32)[None, :]).astype(F32)
    highest = lax.Precision.HIGHEST
    return (jnp.dot(select, mixing, precision=highest), jnp.dot(select, beams, precision=highest))


def quarter_turns(m_order):
    m_lane = jnp.broadcast_to(m_order.reshape(BLOCKS, 1, M_DEV), (BLOCKS, 2, M_DEV))
    part = jnp.array([1.0, -1.0], F32)[None, :, None]
    phase = m_lane % 4
    sign = jnp.where(phase % 2 == 0, 1.0, -1.0).astype(F32)
    cosine = jnp.where(phase == 0, 1.0, jnp.where(phase == 2, -1.0, 0.0)).astype(F32)
    sine = jnp.where(phase == 1, 1.0, jnp.where(phase == 3, -1.0, 0.0)).astype(F32) * part
    rows = jnp.stack([sign, cosine, sine]).reshape(3, 2 * MODES)
    return jnp.concatenate([rows, jnp.zeros((5, 2 * MODES), F32)])


def on_device(
    solution,
    residual,
    direction,
    precond,
    inv_spec,
    mixing,
    beams,
    slot_band,
    m_order,
    cycle_order,
    inv_noise,
    pix_mask,
):
    band_index = lax.axis_index("band")
    block_index = lax.axis_index(BLK)
    cycle_mult = jnp.broadcast_to((2 * cycle_order + 1)[:, None], (CYCLES, 128))
    order_mult = jnp.broadcast_to(m_order[:, None], (MODES, 128))
    turns = quarter_turns(m_order)
    my_orders = lax.dynamic_slice_in_dim(m_order, block_index * M_DEV, M_DEV)
    orders = jnp.broadcast_to(my_orders[:, None], (M_DEV, 128))
    my_slots = lax.dynamic_slice_in_dim(slot_band, band_index * SLOTS, SLOTS)
    slot_mix, slot_beam = slot_tables(my_slots, mixing, beams)
    applied, sums = operator(
        direction,
        residual,
        inv_noise,
        pix_mask,
        cycle_mult,
        order_mult,
        turns,
        orders,
        slot_beam,
        precond,
        inv_spec,
        slot_mix,
    )
    precond_full = precond[:, None, None, :]
    norm_old, curvature, crossed, squared = (sums[index, 0] for index in range(4))
    step_size = norm_old / curvature
    solution_next = solution + step_size * direction
    residual_next = residual - step_size * applied
    scaled_next = precond_full * residual_next
    norm_new = norm_old - 2.0 * step_size * crossed + step_size * step_size * squared
    direction_next = scaled_next + norm_new / norm_old * direction
    return (solution_next, residual_next, direction_next)


def solution(mesh):
    finer = Mesh(
        mesh.devices.reshape(mesh.shape["band"], 8, 4, 2), ("band", "blk_0", "blk_1", "blk_2")
    )
    in_specs = (
        P(None, None, BLK, "band"),
        P(None, None, BLK, "band"),
        P(None, None, BLK, "band"),
        P(None, "band"),
        P(None, "band"),
        P(),
        P(),
        P(),
        P(),
        P(),
        P("band", None, BLK, None),
        P(BLK, None),
    )
    out_specs = (P(None, None, BLK, "band"), P(None, None, BLK, "band"), P(None, None, BLK, "band"))
    return jax.shard_map(
        on_device, mesh=finer, in_specs=in_specs, out_specs=out_specs, check_vma=False
    )
```

time: 295 us -> 184 us (0.62)
  blocking collectives: 147 us -> 0 us
  Pallas kernels: 57.3 us -> 164 us
  waiting for transfers between devices: 44.3 us -> 0 us
  starting transfers between devices: 19.6 us -> 0 us
  other arithmetic: 11.3 us -> 5.48 us
    pallas_call x4 -> x1, Pallas kernels: 57.3 us -> 164 us  [operator(): pl.pallas_call(operator_kernel, in_specs=[pl.BlockSpec(memory_space=pl.AN...]
    psum x1 -> x0, blocking collectives: 75.3 us -> none  [on_device(): norm_old, curvature, crossed, squared = lax.psum(sums, BAND_BLK)]
    all_to_all x2 -> x0, blocking collectives: 71.3 us -> none  [the longest x1 40.1 us: on_device(): lax.all_to_all(weighted_back, BLK, split_axis=0, concat_axis=0, tiled=True)]
    all_to_all x2 -> x0, waiting for transfers between devices: 44.3 us -> none  [the longest x1 32.3 us: on_device(): lax.all_to_all(colat_side.reshape(BLOCKS, R_DEV, LANES), BLK, split_axis=...]
    all_to_all x2 -> x0, starting transfers between devices: 19.6 us -> none  [the longest x1 14.6 us: on_device(): lax.all_to_all(colat_side.reshape(BLOCKS, R_DEV, LANES), BLK, split_axis=...]
  transfers between devices with their start and end apart: 2 -> 0, of which waited for: 2 -> 0; matrix products, arithmetic and copies ran while one was open for 2% -> 0% of each run, Pallas kernels for 4% -> 0%
where the time goes in v2:
time: 184 us
  Pallas kernels  164 us (89%)
  local copies, waits for them, and re-layouts  7.7 us (4%)
  other arithmetic  5.48 us (3%)
  between operations  4.79 us (3%)
  matrix products  2.29 us (1%)
    pallas_call x1, Pallas kernels, operator(): pl.pallas_call(operator_kernel, in_specs=[pl.BlockSpec(memory_space=pl.AN...  164 us
    add x1, other arithmetic, on_device(): direction_next = scaled_next + norm_new / norm_old * direction  3.88 us

profile of v2, /device:TPU:1, one launch (start us, length us, event | category | flops | bytes accessed | tf_op | source)
XLA Modules:
  0.0 183.9 jit_solution(2330812115395363632)
XLA Ops:
  0.6 0.0 copy-start
  0.6 0.0 copy-start.4
  0.7 0.8 dynamic_slice.6
  1.5 0.7 dynamic_slice.7
  2.2 1.5 fusion.3.mix
  3.7 0.7 multiply_add_fusion.2
  4.4 0.7 broadcast_in_dim.60.orders
  5.0 0.0 copy-done
  5.0 0.8 fusion.4.beam
  5.9 0.8 broadcast_in_dim.53
  6.7 0.1 broadcast_select_fusion
  6.7 0.1 select_n.104
  6.9 0.7 mul.71
  7.6 0.1 mul.72
  7.7 0.1 compare_select_fusion.6
  7.8 0.7 select_maximum_fusion.turns
  8.6 1.0 broadcast_in_dim.51.cycle_mult
  9.6 0.0 copy-done.4
  9.6 1.3 broadcast_in_dim.52.order_mult
  10.9 163.7 %operator.1 = (f32[9,2,32,512]{3,2,1,0:T(8,128)}, f32[8,128]{1,0:T(8,128)}) custom-call(f32[9,2,32,512]{3,2,1,0:T(8,128)} %direction_in.1, f32[9,2,32,512]{3,2,1,0:T(8,128)} %residual_in.1, f32[3,3,16,4096]{3,2,1,0:T(8,128)} %noise_in.1, s32[16,4096]{1,0:T(8,128)} %mask_in.1, s32[1024,128]{1,0:T(8,128)} %broadcast_in_dim.51.cycle_mult, ...), custom_call_target="tpu_custom_call" | custom-call | tf_op jit(solution)/shard_map/operator/pallas_call | solution.py:553
  174.5 1.4 fusion.7
  180.0 0.0 copy-done.1
  180.0 0.0 copy-done.2
  180.0 3.9 %multiply_add_fusion = (f32[9,2,32,512]{3,2,1,0:T(8,128)}, f32[9,2,32,512]{3,2,1,0:T(8,128)}, f32[9,2,32,512]{3,2,1,0:T(8,128)}) fusion(f32[9,2,32,512]{3,2,1,0:T(8,128)S(1)} %copy-done.1, f32[]{:T(128)S(6)} %div.7, f32[9,512]{1,0:T(8,128)S(1)} %copy-done.3, f32[9,2,32,512]{3,2,1,0:T(8,128)S(1)} %copy-done.2, f32[9,2,32,512]{3,2,1,0:T(8,128)} %get-tuple-element.6, ...), kind=kLoop, calls=%fused_computation | loop fusion | flops 2064384 | bytes 8275976 | tf_op jit(solution)/shard_map/add | solution.py:662
  (6 shorter events, 0.0 us)
Async XLA Ops:
  0.6 4.4 %copy-start = (f32[9,2048]{1,0:T(8,128)S(1)}, f32[9,2048]{1,0:T(8,128)}, u32[]{:S(2)}) copy-start(f32[9,2048]{1,0:T(8,128)} %param.19) | copy-start | bytes 221188
  0.6 8.9 %copy-start.4 = (s32[2048]{0:T(1024)S(1)}, s32[2048]{0:T(1024)}, u32[]{:S(2)}) copy-start(s32[2048]{0:T(1024)} %param.21) | copy-start | bytes 24580
  10.9 169.1 %copy-start.1 = (f32[9,2,32,512]{3,2,1,0:T(8,128)S(1)}, f32[9,2,32,512]{3,2,1,0:T(8,128)}, u32[]{:S(2)}) copy-start(f32[9,2,32,512]{3,2,1,0:T(8,128)} %direction_in.1) | copy-start | bytes 3538948
  10.9 169.2 %copy-start.2 = (f32[9,2,32,512]{3,2,1,0:T(8,128)S(1)}, f32[9,2,32,512]{3,2,1,0:T(8,128)}, u32[]{:S(2)}) copy-start(f32[9,2,32,512]{3,2,1,0:T(8,128)} %residual_in.1) | copy-start | bytes 3538948
  10.9 169.2 %copy-start.3 = (f32[9,512]{1,0:T(8,128)S(1)}, f32[9,512]{1,0:T(8,128)}, u32[]{:S(2)}) copy-start(f32[9,512]{1,0:T(8,128)} %precond.1) | copy-start | bytes 55300

commit v3 on v2

--- a/solution.py
+++ b/solution.py
@@ -80,9 +80,27 @@
         cosine, sine = cosine * step_cos - sine * step_sin, sine * step_cos + cosine * step_sin
 
 
-def at_least(orders, first, width):
-    l_values = first + lax.broadcasted_iota(jnp.int32, (M_DEV, width), 1)
-    return (l_values >= orders).astype(F32)
+STEP = 32
+
+
+def azim_columns(order, first_turn, store):
+    cell = lax.broadcasted_iota(jnp.int32, (STEP, 128), 0)
+    cosine, sine = unit_circle((order * cell + first_turn) & 4095)
+    step_cos, step_sin = unit_circle((order * STEP) & 4095)
+    cosine, sine = cosine * SCALE, sine * SCALE
+    for step in range(QUARTER // STEP):
+        store(step, cosine.astype(BF16))
+        cosine, sine = cosine * step_cos - sine * step_sin, sine * step_cos + cosine * step_sin
+
+
+def spread(values, row):
+    line = values[pl.ds(row, 1), :].astype(F32)
+    return jnp.broadcast_to(line, (128, 128)).T.astype(jnp.int32)
+
+
+def at_least(orders, first):
+    l_values = first + lax.broadcasted_iota(jnp.int32, (M_DEV, 256), 1)
+    return (l_values >= jnp.concatenate([orders, orders], axis=1)).astype(F32)
 
 
 def partner(value, low):
@@ -105,14 +123,13 @@
     residual_in,
     noise_in,
     mask_in,
-    cycle_mult,
-    order_mult,
-    turns,
-    orders,
-    beam,
+    m_rows,
+    cycle_rows,
+    beams,
     precond,
     inv_spec,
-    mix,
+    mixing,
+    slot_band,
     applied,
     sums,
     direction,
@@ -122,6 +139,11 @@
     gathered,
     colat,
     azim,
+    azim_across,
+    turns,
+    order_lanes,
+    orders,
+    beam,
     amps,
     there,
     there_mid,
@@ -183,8 +205,8 @@
 
     sent = []
 
-    def send(source, target, send_sem, recv_sem, peer):
-        copy = pltpu.make_async_remote_copy(
+    def describe(source, target, send_sem, recv_sem, peer):
+        return pltpu.make_async_remote_copy(
             src_ref=source,
             dst_ref=target,
             send_sem=send_sem,
@@ -192,6 +214,9 @@
             device_id=peer,
             device_id_type=MESH,
         )
+
+    def send(*ends):
+        copy = describe(*ends)
         copy.start()
         sent.append(copy)
         return copy
@@ -200,30 +225,24 @@
         for copy in copies:
             copy.wait_recv()
 
-    loads[0].wait()
-    for s in range(STOKES):
+    def halve(s):
         for k in range(2):
             for c in range(COMP):
                 gathered[s, x_me, k, c] = direction[c * 3 + s, k].astype(BF16)
-        if s == 0:
-            pl.semaphore_wait(barrier, len(peers))
-        if s == 0:
-            direct = []
-        direct.append(
-            [
-                send(
-                    gathered.at[s, x_me],
-                    gathered.at[s, x_me],
-                    gather_send.at[s, way],
-                    gather_recv.at[s, way],
-                    at_x(peer),
-                )
-                for way, peer in enumerate((right, left))
-            ]
-        )
+
+    def gather(s):
+        return [
+            send(
+                gathered.at[s, x_me],
+                gathered.at[s, x_me],
+                gather_send.at[s, way],
+                gather_recv.at[s, way],
+                at_x(peer),
+            )
+            for way, peer in enumerate((right, left))
+        ]
 
     def forward_on(s):
-        arrive(direct[s])
         return [
             send(
                 gathered.at[s, source, way],
@@ -236,27 +255,84 @@
         ]
 
     def make_colat():
-        @pl.loop(0, CYCLES // 32)
+        @pl.loop(0, CYCLES // 128)
         def _(block):
-            rows = pl.ds(pl.multiple_of(block * 32, 32), 32)
-
-            def put(tile, value):
-                colat[rows, tile * 128 : (tile + 1) * 128] = value
-
-            colat_rows(cycle_mult[rows, :], put)
-
-    def make_azim():
-        @pl.loop(0, BLOCKS)
+            mult = 2 * spread(cycle_rows, block) + 1
+            for sub in range(4):
+                rows = pl.ds(pl.multiple_of(block * 128 + sub * 32, 32), 32)
+
+                def put(tile, value):
+                    colat[rows, tile * 128 : (tile + 1) * 128] = value
+
+                colat_rows(mult[sub * 32 : sub * 32 + 32], put)
+
+    def make_azim(begin, end):
+        @pl.loop(begin, end)
         def _(block):
-            rows = pl.ds(pl.multiple_of(block * 32, 32), 32)
-            real_rows = pl.ds(pl.multiple_of(block * 64, 32), 32)
-            imag_rows = pl.ds(pl.multiple_of(block * 64 + 32, 32), 32)
-
-            def put(tile, real, imag):
-                azim[real_rows, tile * 128 : (tile + 1) * 128] = real
-                azim[imag_rows, tile * 128 : (tile + 1) * 128] = imag
-
-            azim_rows(order_mult[rows, :], put)
+            mult = spread(m_rows, block)
+            for sub in range(4):
+                first = block * 256 + sub * 64
+                real_rows = pl.ds(pl.multiple_of(first, 32), 32)
+                imag_rows = pl.ds(pl.multiple_of(first + 32, 32), 32)
+
+                def put(tile, real, imag):
+                    azim[real_rows, tile * 128 : (tile + 1) * 128] = real
+                    azim[imag_rows, tile * 128 : (tile + 1) * 128] = imag
+
+                azim_rows(mult[sub * 32 : sub * 32 + 32], put)
+
+    def make_azim_across(begin, end):
+        @pl.loop(begin, end)
+        def _(tile):
+            cols = pl.ds(pl.multiple_of(tile * 128, 128), 128)
+            order = order_lanes[tile % 2, pl.ds(tile // 2, 1), :]
+            part = lax.broadcasted_iota(jnp.int32, (1, 128), 1) & 32
+
+            def put(step, value):
+                azim_across[step * STEP : (step + 1) * STEP, cols] = value
+
+            azim_columns(order, part * 32, put)
+
+    mix = [[None] * COMP for _ in range(SLOTS)]
+    for x in range(SLOTS):
+        slot = slot_band[x_me * SLOTS + x]
+        for c in range(COMP):
+            mix[x][c] = jnp.where(slot < BANDS, mixing[jnp.minimum(slot, BANDS - 1), c], 0.0)
+
+    def make_small():
+        place = lax.broadcasted_iota(jnp.int32, (16, 128), 1)
+        line = m_rows[...]
+        even = jnp.where(
+            place < 32, line, jnp.where(place < 96, pltpu.roll(line, 32, 1), pltpu.roll(line, 64, 1))
+        )
+        odd = jnp.where(
+            place < 32, pltpu.roll(line, 64, 1), jnp.where(place < 96, pltpu.roll(line, 96, 1), line)
+        )
+        way = jnp.where((place & 63) < 32, 1.0, -1.0)
+        for parity, value in enumerate((even, odd)):
+            order_lanes[parity] = value
+            phase = value & 3
+            turns[0, parity] = jnp.where((value & 1) == 0, 1.0, -1.0)
+            turns[1, parity] = jnp.where(phase == 0, 1.0, jnp.where(phase == 2, -1.0, 0.0))
+            turns[2, parity] = way * jnp.where(
+                phase == 1, 1.0, jnp.where(phase == 3, -1.0, 0.0)
+            )
+        for x in range(SLOTS):
+            slot = slot_band[x_me * SLOTS + x]
+            total = jnp.zeros((1, L), F32)
+            for band in range(BANDS):
+                total = jnp.where(slot == band, beams[band : band + 1, :], total)
+            beam[x : x + 1, :] = total
+        blk = z_me * 8 + y_me
+        all_orders = spread(m_rows, lax.div(blk, 4))
+        for sub in range(4):
+
+            @pl.when(lax.rem(blk, 4) == sub)
+            def _():
+                orders[...] = all_orders[sub * 32 : sub * 32 + 32]
+
+    def turns_of(tile):
+        return [turns[index, tile % 2, pl.ds(tile // 2, 1), :] for index in range(3)]
 
     lane = lax.broadcasted_iota(jnp.int32, (R_DEV, 128), 1)
     on_left = lane < 64
@@ -269,13 +345,13 @@
             first = pl.multiple_of(block * 256, 256)
             piece = block // 2
             inner = pl.ds(pl.multiple_of((block % 2) * 256, 256), 256)
-            triangle = at_least(orders[:, 0:1], first, 256)
+            triangle = at_least(orders[...], first)
             for k in range(2):
                 comps = [gathered[s, piece, k, c, :, inner].astype(F32) for c in range(COMP)]
                 for x in range(SLOTS):
-                    mixed = mix[x, 0] * comps[0]
+                    mixed = mix[x][0] * comps[0]
                     for c in range(1, COMP):
-                        mixed = mixed + mix[x, c] * comps[c]
+                        mixed = mixed + mix[x][c] * comps[c]
                     row = (x * 2 + k) * M_DEV
                     value = mixed * beam[x : x + 1, pl.ds(first, 256)] * triangle
                     amps[row : row + M_DEV, pl.ds(first, 256)] = value.astype(BF16)
@@ -295,39 +371,50 @@
             there[s, pl.ds(block * 2, 2), :, 0:16, :] = main.astype(BF16)
             there[s, pl.ds(block * 2, 2), :, 16:24, :] = packed.reshape(2, 8, 8, 128).astype(BF16)
 
+    def z_copy(way, s, off, source, middle):
+        other = lax.rem(z_me + off, 8)
+        return describe(
+            source.at[s, other],
+            middle.at[s, z_me],
+            z_send.at[way, s, off - 1],
+            z_recv.at[way, s, off - 1],
+            at_z(other),
+        )
+
     def start_z(way, s, source, middle):
-        copies = [
-            send(
-                source.at[s, other],
-                middle.at[s, z_me],
-                z_send.at[way, s, index],
-                z_recv.at[way, s, index],
-                at_z(other),
-            )
-            for index, other in enumerate(z_others)
-        ]
-        middle[s, z_me] = source[s, z_me]
-        return copies
-
-    def start_y(way, s, middle, target):
-        copies = [
-            send(
-                middle.at[s, :, other],
-                target.at[s, :, y_me],
-                y_send.at[way, s, index],
-                y_recv.at[way, s, index],
-                at_y(other),
-            )
-            for index, other in enumerate(y_others)
-        ]
-        target[s, :, y_me] = middle[s, :, y_me]
-        return copies
+        for off in (1, 7, 2, 6, 3, 5, 4):
+            z_copy(way, s, off, source, middle).start()
+
+    def y_copy(way, s, index, source, target):
+        return describe(
+            source, target, y_send.at[way, s, index], y_recv.at[way, s, index], at_y(y_others[index])
+        )
+
+    def pass_on(way, s, source, middle, target):
+        for off in (0, 1, 7, 2, 6, 3, 5, 4):
+            plane = lax.rem(z_me + 8 - off, 8)
+            held = source if off == 0 else middle
+            if off:
+                copy = z_copy(way, s, off, source, middle)
+                copy.wait_recv()
+                sent.append(copy)
+            for index, other in enumerate(y_others):
+                y_copy(
+                    way, s, index, held.at[s, plane, other], target.at[s, plane, y_me]
+                ).start()
+            target[s, plane, y_me] = held[s, plane, y_me]
+
+    def wait_y(way, s, middle, target):
+        for index, other in enumerate(y_others):
+            copy = y_copy(way, s, index, middle.at[s, :, other], target.at[s, :, y_me])
+            copy.wait_recv()
+            sent.append(copy)
 
     def azimuth(s):
-        @pl.loop(0, BLOCKS // 2)
+        @pl.loop(0, BLOCKS // 2, unroll=4)
         def _(tile):
             cols = pl.ds(pl.multiple_of(tile * 128, 128), 128)
-            sign, cosine, sine = turns[0:1, cols], turns[1:2, cols], turns[2:3, cols]
+            sign, cosine, sine = turns_of(tile)
             plane, place = tile // 4, (tile % 4) * 2
             first = arrived[s, plane, place, 0:16, :].astype(F32)
             second = arrived[s, plane, place + 1, 0:16, :].astype(F32)
@@ -368,14 +455,21 @@
                         weight * sky[row : row + R_DEV, :]
                     ).astype(BF16)
 
-        @pl.loop(0, BLOCKS // 4)
-        def _(block):
-            rows = pl.ds(pl.multiple_of(block * 256, 256), 256)
-            back = lax.dot_general(weighted[...], azim[rows, :], NT, preferred_element_type=F32)
-            for sub in range(2):
-                tile = block * 2 + sub
-                cols = pl.ds(pl.multiple_of(tile * 128, 128), 128)
-                sign, cosine, sine = turns[0:1, cols], turns[1:2, cols], turns[2:3, cols]
+        @pl.loop(1, 9)
+        def _(off):
+            home_plane = lax.rem(z_me + off, 8)
+            backs = []
+            for half in range(2):
+                cols = pl.ds(pl.multiple_of(home_plane * 512 + half * 256, 256), 256)
+                backs.append(
+                    lax.dot_general(
+                        weighted[...], azim_across[:, cols], NN, preferred_element_type=F32
+                    )
+                )
+            for inner in range(4):
+                tile = home_plane * 4 + inner
+                back, sub = backs[inner // 2], inner % 2
+                sign, cosine, sine = turns_of(tile)
                 lanes = slice(sub * 128, sub * 128 + 128)
                 values = []
                 for x in range(SLOTS):
@@ -387,7 +481,7 @@
                         b0 + sign * b2 + cosine * (b1 + b3) + sine * partner(b1 - b3, low)
                     )
                 zero, one, two = values
-                plane, place = tile // 4, (tile % 4) * 2
+                plane, place = home_plane, inner * 2
                 home[s, plane, place, 0:16, :] = jnp.where(
                     on_left, zero, pltpu.roll(one, 64, 1)
                 ).astype(BF16)
@@ -401,6 +495,10 @@
                     on_left8, pltpu.roll(two[:8], 64, 1), two[8:]
                 ).astype(BF16)
 
+            @pl.when(off < 8)
+            def _():
+                z_copy(1, s, off, home, home_mid).start()
+
     def legendre_back(s):
         @pl.loop(0, 8)
         def _(plane):
@@ -419,7 +517,7 @@
             harm = lax.dot_general(
                 flipped[0:192, :], colat[:, cols], NN, preferred_element_type=F32
             )
-            triangle = at_least(orders[:, 0:1], start, 256)
+            triangle = at_least(orders[...], start)
             piece = block // 2
             inner = pl.ds(pl.multiple_of((block % 2) * 256, 256), 256)
             for k in range(2):
@@ -428,9 +526,9 @@
                     row = (x * 2 + k) * M_DEV
                     shaped.append(harm[row : row + M_DEV, :] * beam[x : x + 1, cols] * triangle)
                 for c in range(COMP):
-                    total = mix[0, c] * shaped[0]
+                    total = mix[0][c] * shaped[0]
                     for x in range(1, SLOTS):
-                        total = total + mix[x, c] * shaped[x]
+                        total = total + mix[x][c] * shaped[x]
                     combined[s, piece, c, k, :, inner] = total.astype(BF16)
 
     def start_x(s):
@@ -479,54 +577,60 @@
         arrive(copies)
         return jnp.sum(buffer[...], axis=0)
 
+    loads[0].wait()
+    halve(0)
+    pl.semaphore_wait(barrier, len(peers))
+    direct = gather(0)
+    halve(1)
+    halve(2)
     totals[...] = jnp.zeros_like(totals)
     amps[192:256, :] = jnp.zeros((64, L), BF16)
+    make_small()
     make_colat()
-    relayed = [forward_on(0)]
+    arrive(direct)
+    relayed = forward_on(0)
+    direct = gather(1)
+    make_azim(0, 8)
+    arrive(relayed)
+    legendre(0)
+    start_z(0, 0, there, there_mid)
+    arrive(direct)
+    relayed = forward_on(1)
+    direct = gather(2)
+    make_azim(8, 16)
+    arrive(relayed)
+    legendre(1)
+    start_z(0, 1, there, there_mid)
+    arrive(direct)
+    relayed = forward_on(2)
+    make_azim_across(0, 16)
+    pass_on(0, 0, there, there_mid, arrived)
+    arrive(relayed)
+    legendre(2)
+    start_z(0, 2, there, there_mid)
+    make_azim_across(16, 32)
     for load in loads[1:]:
         load.wait()
-    arrive(relayed[0])
-    legendre(0)
-    z_there = [start_z(0, 0, there, there_mid)]
-    relayed.append(forward_on(1))
-    make_azim()
-    relayed.append(forward_on(2))
-    arrive(relayed[1])
-    legendre(1)
-    z_there.append(start_z(0, 1, there, there_mid))
-    arrive(z_there[0])
-    y_there = [start_y(0, 0, there_mid, arrived)]
-    arrive(relayed[2])
-    legendre(2)
-    z_there.append(start_z(0, 2, there, there_mid))
-    arrive(y_there[0])
+    wait_y(0, 0, there_mid, arrived)
     azimuth(0)
-    z_home = [start_z(1, 0, home, home_mid)]
-    arrive(z_there[1])
-    y_there.append(start_y(0, 1, there_mid, arrived))
-    arrive(y_there[1])
+    pass_on(0, 1, there, there_mid, arrived)
+    wait_y(0, 1, there_mid, arrived)
     azimuth(1)
-    z_home.append(start_z(1, 1, home, home_mid))
-    arrive(z_there[2])
-    y_there.append(start_y(0, 2, there_mid, arrived))
-    arrive(y_there[2])
+    pass_on(0, 2, there, there_mid, arrived)
+    wait_y(0, 2, there_mid, arrived)
     azimuth(2)
-    z_home.append(start_z(1, 2, home, home_mid))
-    arrive(z_home[0])
-    y_home = [start_y(1, 0, home_mid, returned)]
-    arrive(y_home[0])
+    pass_on(1, 0, home, home_mid, returned)
+    wait_y(1, 0, home_mid, returned)
     legendre_back(0)
     x_home = [start_x(0)]
-    arrive(z_home[1])
-    y_home.append(start_y(1, 1, home_mid, returned))
-    arrive(y_home[1])
+    pass_on(1, 1, home, home_mid, returned)
+    wait_y(1, 1, home_mid, returned)
     legendre_back(1)
     x_home.append(start_x(1))
-    arrive(z_home[2])
-    y_home.append(start_y(1, 2, home_mid, returned))
     arrive(x_home[0])
     apply(0)
-    arrive(y_home[2])
+    pass_on(1, 2, home, home_mid, returned)
+    wait_y(1, 2, home_mid, returned)
     legendre_back(2)
     x_home.append(start_x(2))
     arrive(x_home[1])
@@ -552,7 +656,7 @@
     local = (FIELDS, 2, M_DEV, L_DEV)
     return pl.pallas_call(
         operator_kernel,
-        in_specs=[pl.BlockSpec(memory_space=pl.ANY)] * 4 + [in_vmem()] * 7 + [in_smem()],
+        in_specs=[pl.BlockSpec(memory_space=pl.ANY)] * 4 + [in_vmem()] * 5 + [in_smem()] * 2,
         out_specs=[in_vmem(), in_vmem()],
         out_shape=[jax.ShapeDtypeStruct(local, F32), jax.ShapeDtypeStruct((8, 128), F32)],
         scratch_shapes=[
@@ -563,6 +667,11 @@
             VMEM((STOKES, 4, 2, COMP, M_DEV, L_DEV), BF16),
             VMEM((CYCLES, L), BF16),
             VMEM((2 * MODES, QUARTER), BF16),
+            VMEM((QUARTER, 2 * MODES), BF16),
+            VMEM((3, 2, 16, 128), F32),
+            VMEM((2, 16, 128), jnp.int32),
+            VMEM((M_DEV, 128), jnp.int32),
+            VMEM((SLOTS, L), F32),
             VMEM((256, L), BF16),
             VMEM(block, BF16),
             VMEM(block, BF16),
@@ -598,21 +707,34 @@
     )(direction, residual, noise, mask, *small)
 
 
-def slot_tables(my_slots, mixing, beams):
-    select = (my_slots[:, None] == jnp.arange(BANDS, dtype=jnp.int32)[None, :]).astype(F32)
-    highest = lax.Precision.HIGHEST
-    return (jnp.dot(select, mixing, precision=highest), jnp.dot(select, beams, precision=highest))
-
-
-def quarter_turns(m_order):
-    m_lane = jnp.broadcast_to(m_order.reshape(BLOCKS, 1, M_DEV), (BLOCKS, 2, M_DEV))
-    part = jnp.array([1.0, -1.0], F32)[None, :, None]
-    phase = m_lane % 4
-    sign = jnp.where(phase % 2 == 0, 1.0, -1.0).astype(F32)
-    cosine = jnp.where(phase == 0, 1.0, jnp.where(phase == 2, -1.0, 0.0)).astype(F32)
-    sine = jnp.where(phase == 1, 1.0, jnp.where(phase == 3, -1.0, 0.0)).astype(F32) * part
-    rows = jnp.stack([sign, cosine, sine]).reshape(3, 2 * MODES)
-    return jnp.concatenate([rows, jnp.zeros((5, 2 * MODES), F32)])
+def finish_kernel(sums, precond, solution, residual, direction, applied, out_sol, out_res, out_dir):
+    norm_old, curvature, crossed, squared = (
+        jnp.concatenate([sums[index : index + 1, :]] * 4, axis=1) for index in range(4)
+    )
+    step_size = norm_old / curvature
+    norm_new = norm_old - 2.0 * step_size * crossed + step_size * step_size * squared
+    ratio = norm_new / norm_old
+    pre = precond[pl.ds(pl.program_id(0), 1), :]
+    for k in range(2):
+        dir_now = direction[0, k]
+        res_next = residual[0, k] - step_size * applied[0, k]
+        out_sol[0, k] = solution[0, k] + step_size * dir_now
+        out_res[0, k] = res_next
+        out_dir[0, k] = pre * res_next + ratio * dir_now
+
+
+def finish(sums, precond, *arrays):
+    local = (FIELDS, 2, M_DEV, L_DEV)
+    field = pl.BlockSpec((1, 2, M_DEV, L_DEV), lambda g: (g, 0, 0, 0))
+    whole = [pl.BlockSpec((8, 128), lambda g: (0, 0)), pl.BlockSpec((FIELDS, L_DEV), lambda g: (0, 0))]
+    return pl.pallas_call(
+        finish_kernel,
+        grid=(FIELDS,),
+        in_specs=whole + [field] * 4,
+        out_specs=[field] * 3,
+        out_shape=[jax.ShapeDtypeStruct(local, F32)] * 3,
+        name="finish",
+    )(sums, precond, *arrays)
 
 
 def on_device(
@@ -629,38 +751,20 @@
     inv_noise,
     pix_mask,
 ):
-    band_index = lax.axis_index("band")
-    block_index = lax.axis_index(BLK)
-    cycle_mult = jnp.broadcast_to((2 * cycle_order + 1)[:, None], (CYCLES, 128))
-    order_mult = jnp.broadcast_to(m_order[:, None], (MODES, 128))
-    turns = quarter_turns(m_order)
-    my_orders = lax.dynamic_slice_in_dim(m_order, block_index * M_DEV, M_DEV)
-    orders = jnp.broadcast_to(my_orders[:, None], (M_DEV, 128))
-    my_slots = lax.dynamic_slice_in_dim(slot_band, band_index * SLOTS, SLOTS)
-    slot_mix, slot_beam = slot_tables(my_slots, mixing, beams)
     applied, sums = operator(
         direction,
         residual,
         inv_noise,
         pix_mask,
-        cycle_mult,
-        order_mult,
-        turns,
-        orders,
-        slot_beam,
+        m_order.reshape(16, 128),
+        cycle_order.reshape(8, 128),
+        beams,
         precond,
         inv_spec,
-        slot_mix,
+        mixing,
+        slot_band,
     )
-    precond_full = precond[:, None, None, :]
-    norm_old, curvature, crossed, squared = (sums[index, 0] for index in range(4))
-    step_size = norm_old / curvature
-    solution_next = solution + step_size * direction
-    residual_next = residual - step_size * applied
-    scaled_next = precond_full * residual_next
-    norm_new = norm_old - 2.0 * step_size * crossed + step_size * step_size * squared
-    direction_next = scaled_next + norm_new / norm_old * direction
-    return (solution_next, residual_next, direction_next)
+    return tuple(finish(sums, precond, solution, residual, direction, applied))
 
 
 def solution(mesh):

time: 184 us -> 148 us (0.80)
  Pallas kernels: 164 us -> 145 us
  local copies, waits for them, and re-layouts: 7.7 us -> 1.36 us
  other arithmetic: 5.48 us -> 0 us
  between operations: 4.79 us -> 0.64 us
  matrix products: 2.29 us -> 0 us
    pallas_call x1, Pallas kernels: 164 us -> 138 us  [operator(): pl.pallas_call(operator_kernel, in_specs=[pl.BlockSpec(memory_space=pl.AN...]
    pallas_call x0 -> x1, Pallas kernels: none -> 7.03 us  [finish(): pl.pallas_call(finish_kernel, grid=(FIELDS,), in_specs=whole + [field] *...]
    add x3 -> x0, other arithmetic: 4.58 us -> none  [the longest x1 3.88 us: on_device(): direction_next = scaled_next + norm_new / norm_old * direction]
    broadcast_in_dim x4 -> x0, local copies, waits for them, and re-layouts: 3.74 us -> none  [the longest x1 1.31 us: on_device(): order_mult = jnp.broadcast_to(m_order[:, None], (MODES, 128))]
    dot_general x2 -> x0, matrix products: 2.29 us -> none  [the longest x1 1.46 us: slot_tables(): jnp.dot(select, mixing, precision=highest)]
where the time goes in v3:
time: 148 us; the launch traced here: 147 us
  Pallas kernels  145 us (98%)
    pallas_call x1, Pallas kernels, operator(): pl.pallas_call(operator_kernel, in_specs=[pl.BlockSpec(memory_space=pl.AN...  138 us
    pallas_call x1, Pallas kernels, finish(): pl.pallas_call(finish_kernel, grid=(FIELDS,), in_specs=whole + [field] *...  7.03 us

profile of v3, /device:TPU:1, one launch (start us, length us, event | category | flops | bytes accessed | tf_op | source)
XLA Modules:
  0.0 147.5 jit_solution(1412960766343192063)
XLA Ops:
  0.6 1.4 copy.15.mixing
  2.0 138.4 %operator.1 = (f32[9,2,32,512]{3,2,1,0:T(8,128)}, f32[8,128]{1,0:T(8,128)}) custom-call(f32[9,2,32,512]{3,2,1,0:T(8,128)} %direction.1, f32[9,2,32,512]{3,2,1,0:T(8,128)} %residual.1, f32[3,3,16,4096]{3,2,1,0:T(8,128)} %noise_in.1, s32[16,4096]{1,0:T(8,128)} %mask_in.1, s32[16,128]{1,0:T(8,128)} %bitcast.2, s32[8,128]{1,0:T(8,128)} %bitcast.3, ...), custom_call_target="tpu_custom_call" | custom-call | tf_op jit(solution)/shard_map/operator/pallas_call | solution.py:657
  140.4 7.0 %finish.1 = (f32[9,2,32,512]{3,2,1,0:T(8,128)}, f32[9,2,32,512]{3,2,1,0:T(8,128)}, f32[9,2,32,512]{3,2,1,0:T(8,128)}) custom-call(f32[8,128]{1,0:T(8,128)} %get-tuple-element.5.sums, f32[9,512]{1,0:T(8,128)} %precond.3, f32[9,2,32,512]{3,2,1,0:T(8,128)} %solution.1, f32[9,2,32,512]{3,2,1,0:T(8,128)} %residual.1, f32[9,2,32,512]{3,2,1,0:T(8,128)} %direction.1, ...), custom_call_target="tpu_custom_call" | custom-call | tf_op jit(solution)/shard_map/finish/pallas_call | solution.py:730

commit v4 on v3

--- a/solution.py
+++ b/solution.py
@@ -297,7 +297,7 @@
     for x in range(SLOTS):
         slot = slot_band[x_me * SLOTS + x]
         for c in range(COMP):
-            mix[x][c] = jnp.where(slot < BANDS, mixing[jnp.minimum(slot, BANDS - 1), c], 0.0)
+            mix[x][c] = jnp.where(slot < BANDS, mixing[c, jnp.minimum(slot, BANDS - 1)], 0.0)
 
     def make_small():
         place = lax.broadcasted_iota(jnp.int32, (16, 128), 1)
@@ -410,7 +410,7 @@
             copy.wait_recv()
             sent.append(copy)
 
-    def azimuth(s):
+    def azimuth(s, between):
         @pl.loop(0, BLOCKS // 2, unroll=4)
         def _(tile):
             cols = pl.ds(pl.multiple_of(tile * 128, 128), 128)
@@ -440,7 +440,7 @@
                     row = q * 48 + x * R_DEV
                     turned[row : row + R_DEV, cols] = part.astype(BF16)
 
-        @pl.loop(0, QUARTER // 256)
+        @pl.loop(0, QUARTER // 256, unroll=2)
         def _(block):
             start = pl.multiple_of(block * 256, 256)
             cols = pl.ds(start, 256)
@@ -454,6 +454,8 @@
                     weighted[row : row + R_DEV, cols] = (
                         weight * sky[row : row + R_DEV, :]
                     ).astype(BF16)
+
+        between()
 
         @pl.loop(1, 9)
         def _(off):
@@ -510,38 +512,53 @@
             flipped[0:128, cols] = main.T.astype(BF16)
             flipped[128:256, cols] = both.T.astype(BF16)
 
-        @pl.loop(0, L // 256)
-        def _(block):
-            start = pl.multiple_of(block * 256, 256)
-            cols = pl.ds(start, 256)
-            harm = lax.dot_general(
-                flipped[0:192, :], colat[:, cols], NN, preferred_element_type=F32
-            )
-            triangle = at_least(orders[...], start)
-            piece = block // 2
-            inner = pl.ds(pl.multiple_of((block % 2) * 256, 256), 256)
-            for k in range(2):
-                shaped = []
-                for x in range(SLOTS):
-                    row = (x * 2 + k) * M_DEV
-                    shaped.append(harm[row : row + M_DEV, :] * beam[x : x + 1, cols] * triangle)
-                for c in range(COMP):
-                    total = mix[0][c] * shaped[0]
-                    for x in range(1, SLOTS):
-                        total = total + mix[x][c] * shaped[x]
-                    combined[s, piece, c, k, :, inner] = total.astype(BF16)
-
-    def start_x(s):
-        return [
-            send(
-                combined.at[s, other],
-                parts.at[s, index],
-                x_send.at[s, index],
-                x_recv.at[s, index],
-                at_x(other),
-            )
-            for index, other in enumerate((right, left, across))
-        ]
+        @pl.loop(1, 5)
+        def _(off):
+            piece = lax.rem(x_me + off, 4)
+            for half in range(2):
+                start = pl.multiple_of(piece * L_DEV + half * 256, 256)
+                harm = lax.dot_general(
+                    flipped[0:192, :],
+                    colat[:, pl.ds(start, 256)],
+                    NN,
+                    preferred_element_type=F32,
+                )
+                triangle = at_least(orders[...], start)
+                inner = slice(half * 256, half * 256 + 256)
+                for k in range(2):
+                    shaped = []
+                    for x in range(SLOTS):
+                        row = (x * 2 + k) * M_DEV
+                        shaped.append(
+                            harm[row : row + M_DEV, :]
+                            * beam[x : x + 1, pl.ds(start, 256)]
+                            * triangle
+                        )
+                    for c in range(COMP):
+                        total = mix[0][c] * shaped[0]
+                        for x in range(1, SLOTS):
+                            total = total + mix[x][c] * shaped[x]
+                        combined[s, piece, c, k, :, inner] = total.astype(BF16)
+
+            @pl.when(off < 4)
+            def _():
+                x_copy(s, off).start()
+
+    def x_copy(s, off):
+        other = lax.rem(x_me + off, 4)
+        return describe(
+            combined.at[s, other],
+            parts.at[s, off - 1],
+            x_send.at[s, off - 1],
+            x_recv.at[s, off - 1],
+            at_x(other),
+        )
+
+    def wait_x(s):
+        for off in range(1, 4):
+            copy = x_copy(s, off)
+            copy.wait_recv()
+            sent.append(copy)
 
     def apply(s):
         for c in range(COMP):
@@ -612,30 +629,28 @@
     for load in loads[1:]:
         load.wait()
     wait_y(0, 0, there_mid, arrived)
-    azimuth(0)
-    pass_on(0, 1, there, there_mid, arrived)
+    azimuth(0, lambda: pass_on(0, 1, there, there_mid, arrived))
     wait_y(0, 1, there_mid, arrived)
-    azimuth(1)
-    pass_on(0, 2, there, there_mid, arrived)
+    azimuth(1, lambda: pass_on(0, 2, there, there_mid, arrived))
+    pass_on(1, 0, home, home_mid, returned)
     wait_y(0, 2, there_mid, arrived)
-    azimuth(2)
-    pass_on(1, 0, home, home_mid, returned)
-    wait_y(1, 0, home_mid, returned)
-    legendre_back(0)
-    x_home = [start_x(0)]
+
+    def first_back():
+        wait_y(1, 0, home_mid, returned)
+        legendre_back(0)
+
+    azimuth(2, first_back)
     pass_on(1, 1, home, home_mid, returned)
     wait_y(1, 1, home_mid, returned)
     legendre_back(1)
-    x_home.append(start_x(1))
-    arrive(x_home[0])
+    pass_on(1, 2, home, home_mid, returned)
+    wait_x(0)
     apply(0)
-    pass_on(1, 2, home, home_mid, returned)
     wait_y(1, 2, home_mid, returned)
     legendre_back(2)
-    x_home.append(start_x(2))
-    arrive(x_home[1])
+    wait_x(1)
     apply(1)
-    arrive(x_home[2])
+    wait_x(2)
     apply(2)
 
     row = lax.broadcasted_iota(jnp.int32, (8, 128), 0)
@@ -714,22 +729,23 @@
     step_size = norm_old / curvature
     norm_new = norm_old - 2.0 * step_size * crossed + step_size * step_size * squared
     ratio = norm_new / norm_old
-    pre = precond[pl.ds(pl.program_id(0), 1), :]
-    for k in range(2):
-        dir_now = direction[0, k]
-        res_next = residual[0, k] - step_size * applied[0, k]
-        out_sol[0, k] = solution[0, k] + step_size * dir_now
-        out_res[0, k] = res_next
-        out_dir[0, k] = pre * res_next + ratio * dir_now
+    for field in range(COMP):
+        pre = precond[pl.ds(pl.program_id(0) * COMP + field, 1), :]
+        for k in range(2):
+            dir_now = direction[field, k]
+            res_next = residual[field, k] - step_size * applied[field, k]
+            out_sol[field, k] = solution[field, k] + step_size * dir_now
+            out_res[field, k] = res_next
+            out_dir[field, k] = pre * res_next + ratio * dir_now
 
 
 def finish(sums, precond, *arrays):
     local = (FIELDS, 2, M_DEV, L_DEV)
-    field = pl.BlockSpec((1, 2, M_DEV, L_DEV), lambda g: (g, 0, 0, 0))
+    field = pl.BlockSpec((COMP, 2, M_DEV, L_DEV), lambda g: (g, 0, 0, 0))
     whole = [pl.BlockSpec((8, 128), lambda g: (0, 0)), pl.BlockSpec((FIELDS, L_DEV), lambda g: (0, 0))]
     return pl.pallas_call(
         finish_kernel,
-        grid=(FIELDS,),
+        grid=(FIELDS // COMP,),
         in_specs=whole + [field] * 4,
         out_specs=[field] * 3,
         out_shape=[jax.ShapeDtypeStruct(local, F32)] * 3,
@@ -761,7 +777,7 @@
         beams,
         precond,
         inv_spec,
-        mixing,
+        mixing.T,
         slot_band,
     )
     return tuple(finish(sums, precond, solution, residual, direction, applied))

time: 148 us -> 125 us (0.84)
  Pallas kernels: 145 us -> 125 us
    pallas_call x1, Pallas kernels: 138 us -> 120 us  [operator(): pl.pallas_call(operator_kernel, in_specs=[pl.BlockSpec(memory_space=pl.AN...]
    pallas_call x1, Pallas kernels: 7.03 us -> 4.92 us  [finish(): pl.pallas_call(finish_kernel, grid=(FIELDS // COMP,), in_specs=whole + [f...]
where the time goes in v4:
time: 125 us
  Pallas kernels  125 us (100%)
    pallas_call x1, Pallas kernels, operator(): pl.pallas_call(operator_kernel, in_specs=[pl.BlockSpec(memory_space=pl.AN...  120 us
    pallas_call x1, Pallas kernels, finish(): pl.pallas_call(finish_kernel, grid=(FIELDS // COMP,), in_specs=whole + [f...  4.92 us

profile of v4, /device:TPU:1, one launch (start us, length us, event | category | flops | bytes accessed | tf_op | source)
XLA Modules:
  0.0 125.2 jit_solution(13004494297026052739)
XLA Ops:
  0.6 119.6 %operator.1 = (f32[9,2,32,512]{3,2,1,0:T(8,128)}, f32[8,128]{1,0:T(8,128)}) custom-call(f32[9,2,32,512]{3,2,1,0:T(8,128)} %direction.1, f32[9,2,32,512]{3,2,1,0:T(8,128)} %residual.1, f32[3,3,16,4096]{3,2,1,0:T(8,128)} %noise_in.1, s32[16,4096]{1,0:T(8,128)} %mask_in.1, s32[16,128]{1,0:T(8,128)} %bitcast.3, s32[8,128]{1,0:T(8,128)} %bitcast.4, ...), custom_call_target="tpu_custom_call" | custom-call | tf_op jit(solution)/shard_map/operator/pallas_call | solution.py:672
  120.3 4.9 %finish.1 = (f32[9,2,32,512]{3,2,1,0:T(8,128)}, f32[9,2,32,512]{3,2,1,0:T(8,128)}, f32[9,2,32,512]{3,2,1,0:T(8,128)}) custom-call(f32[8,128]{1,0:T(8,128)} %get-tuple-element.5.sums, f32[9,512]{1,0:T(8,128)} %precond.3, f32[9,2,32,512]{3,2,1,0:T(8,128)} %solution.1, f32[9,2,32,512]{3,2,1,0:T(8,128)} %residual.1, f32[9,2,32,512]{3,2,1,0:T(8,128)} %direction.1, ...), custom_call_target="tpu_custom_call" | custom-call | tf_op jit(solution)/shard_map/finish/pallas_call | solution.py:746

commit v5 on v4

--- a/solution.py
+++ b/solution.py
@@ -638,9 +638,9 @@
     def first_back():
         wait_y(1, 0, home_mid, returned)
         legendre_back(0)
+        pass_on(1, 1, home, home_mid, returned)
 
     azimuth(2, first_back)
-    pass_on(1, 1, home, home_mid, returned)
     wait_y(1, 1, home_mid, returned)
     legendre_back(1)
     pass_on(1, 2, home, home_mid, returned)

time: 125 us -> 123 us (0.984)
  Pallas kernels: 125 us -> 122 us
    pallas_call x1, Pallas kernels: 120 us -> 117 us  [operator(): pl.pallas_call(operator_kernel, in_specs=[pl.BlockSpec(memory_space=pl.AN...]
where the time goes in v5:
time: 123 us
  Pallas kernels  122 us (99%)
    pallas_call x1, Pallas kernels, operator(): pl.pallas_call(operator_kernel, in_specs=[pl.BlockSpec(memory_space=pl.AN...  117 us
    pallas_call x1, Pallas kernels, finish(): pl.pallas_call(finish_kernel, grid=(FIELDS // COMP,), in_specs=whole + [f...  4.92 us

profile of v5, /device:TPU:1, one launch (start us, length us, event | category | flops | bytes accessed | tf_op | source)
XLA Modules:
  0.0 122.9 jit_solution(8809929172889074090)
XLA Ops:
  0.6 117.3 %operator.1 = (f32[9,2,32,512]{3,2,1,0:T(8,128)}, f32[8,128]{1,0:T(8,128)}) custom-call(f32[9,2,32,512]{3,2,1,0:T(8,128)} %direction.1, f32[9,2,32,512]{3,2,1,0:T(8,128)} %residual.1, f32[3,3,16,4096]{3,2,1,0:T(8,128)} %noise_in.1, s32[16,4096]{1,0:T(8,128)} %mask_in.1, s32[16,128]{1,0:T(8,128)} %bitcast.3, s32[8,128]{1,0:T(8,128)} %bitcast.4, ...), custom_call_target="tpu_custom_call" | custom-call | tf_op jit(solution)/shard_map/operator/pallas_call | solution.py:672
  117.9 4.9 %finish.1 = (f32[9,2,32,512]{3,2,1,0:T(8,128)}, f32[9,2,32,512]{3,2,1,0:T(8,128)}, f32[9,2,32,512]{3,2,1,0:T(8,128)}) custom-call(f32[8,128]{1,0:T(8,128)} %get-tuple-element.5.sums, f32[9,512]{1,0:T(8,128)} %precond.3, f32[9,2,32,512]{3,2,1,0:T(8,128)} %solution.1, f32[9,2,32,512]{3,2,1,0:T(8,128)} %residual.1, f32[9,2,32,512]{3,2,1,0:T(8,128)} %direction.1, ...), custom_call_target="tpu_custom_call" | custom-call | tf_op jit(solution)/shard_map/finish/pallas_call | solution.py:746

commit v6 on v5

--- a/solution.py
+++ b/solution.py
@@ -340,7 +340,7 @@
     low = (lane & 63) < 32
 
     def legendre(s):
-        @pl.loop(0, L // 256)
+        @pl.loop(0, L // 256, unroll=2)
         def _(block):
             first = pl.multiple_of(block * 256, 256)
             piece = block // 2
@@ -356,7 +356,7 @@
                     value = mixed * beam[x : x + 1, pl.ds(first, 256)] * triangle
                     amps[row : row + M_DEV, pl.ds(first, 256)] = value.astype(BF16)
 
-        @pl.loop(0, CYCLES // 256)
+        @pl.loop(0, CYCLES // 256, unroll=2)
         def _(block):
             rows = pl.ds(pl.multiple_of(block * 256, 256), 256)
             side = lax.dot_general(colat[rows, :], amps[...], NT, preferred_element_type=F32)
@@ -502,7 +502,7 @@
                 z_copy(1, s, off, home, home_mid).start()
 
     def legendre_back(s):
-        @pl.loop(0, 8)
+        @pl.loop(0, 8, unroll=4)
         def _(plane):
             cols = pl.ds(pl.multiple_of(plane * 128, 128), 128)
             main = returned[s, plane, :, 0:16, :].astype(F32).reshape(128, 128)

time: 123 us -> 120 us (0.976)
  Pallas kernels: 122 us -> 120 us
    pallas_call x1, Pallas kernels: 117 us -> 115 us  [operator(): pl.pallas_call(operator_kernel, in_specs=[pl.BlockSpec(memory_space=pl.AN...]
where the time goes in v6:
time: 120 us
  Pallas kernels  120 us (100%)
    pallas_call x1, Pallas kernels, operator(): pl.pallas_call(operator_kernel, in_specs=[pl.BlockSpec(memory_space=pl.AN...  115 us
    pallas_call x1, Pallas kernels, finish(): pl.pallas_call(finish_kernel, grid=(FIELDS // COMP,), in_specs=whole + [f...  4.92 us

profile of v6, /device:TPU:1, one launch (start us, length us, event | category | flops | bytes accessed | tf_op | source)
XLA Modules:
  0.0 120.2 jit_solution(2983115617139696789)
XLA Ops:
  0.6 114.7 %operator.1 = (f32[9,2,32,512]{3,2,1,0:T(8,128)}, f32[8,128]{1,0:T(8,128)}) custom-call(f32[9,2,32,512]{3,2,1,0:T(8,128)} %direction.1, f32[9,2,32,512]{3,2,1,0:T(8,128)} %residual.1, f32[3,3,16,4096]{3,2,1,0:T(8,128)} %noise_in.1, s32[16,4096]{1,0:T(8,128)} %mask_in.1, s32[16,128]{1,0:T(8,128)} %bitcast.3, s32[8,128]{1,0:T(8,128)} %bitcast.4, ...), custom_call_target="tpu_custom_call" | custom-call | tf_op jit(solution)/shard_map/operator/pallas_call | solution.py:672
  115.3 4.9 %finish.1 = (f32[9,2,32,512]{3,2,1,0:T(8,128)}, f32[9,2,32,512]{3,2,1,0:T(8,128)}, f32[9,2,32,512]{3,2,1,0:T(8,128)}) custom-call(f32[8,128]{1,0:T(8,128)} %get-tuple-element.5.sums, f32[9,512]{1,0:T(8,128)} %precond.3, f32[9,2,32,512]{3,2,1,0:T(8,128)} %solution.1, f32[9,2,32,512]{3,2,1,0:T(8,128)} %residual.1, f32[9,2,32,512]{3,2,1,0:T(8,128)} %direction.1, ...), custom_call_target="tpu_custom_call" | custom-call | tf_op jit(solution)/shard_map/finish/pallas_call | solution.py:746
